TPU v7x, 768 devices: a whole 4x8x12 slice. The times are simulated.
768 devices in a mesh: dp: 24 (over z, x_hi), expert: 32 (over y, x_lo, core).
Axes of the slice: x: 4 (x_hi: 2, x_lo: 2; x = x_hi * 2 + x_lo), y: 8, z: 12, core: 2. Of those that a mesh axis runs over, the one named last changes fastest.
Arguments:
- grad_output: bfloat16 [32, 48, 3840], P('expert', None, 'dp'), may hold values from -6 to 6
- router_logits: float32 [32, 48, 128], P('expert'), may hold values from -8 to 8
- expert_ids: int32 [32, 48, 8], P('expert'), may hold values from 0 to 127, all different within a row; in each aligned block of 48 rows (0 to 47, 48 to 95, ..., all dimensions but the last counted through in order) at most 6 rows name the same one
- router_input: bfloat16 [32, 48, 3840], P('expert', 'dp'), may hold values from -6 to 6
- router_weight: bfloat16 [128, 3840], P(None, 'dp'), may hold values from -0.09375 to 0.09375
- gate_weight: bfloat16 [128, 3840, 1024], P('expert', 'dp'), may hold values from -0.09375 to 0.09375
- up_weight: bfloat16 [128, 3840, 1024], P('expert', 'dp'), may hold values from -0.09375 to 0.09375
- down_weight: bfloat16 [128, 1024, 3840], P('expert', None, 'dp'), may hold values from -0.1875 to 0.1875
- gate_saved: bfloat16 [128, 192, 1024], P('expert'), may hold values from -6 to 6
- up_saved: bfloat16 [128, 192, 1024], P('expert'), may hold values from -6 to 6
Outputs:
- grad_input: bfloat16 [32, 48, 3840], P('expert', None, 'dp')
- grad_router: float32 [128, 3840], P('expert', 'dp')
Inputs may be any that keep to these rules, and one draw needn't show every extreme that they name: `expert_ids`: within one token group (the 48 tokens of one index of expert, in order), no expert is named more than 6 times, a bound that some block reaches; every row names 8 different experts.
All inputs are finite; a program needn't handle non-finite values.
Results may differ from a plain program's by a relative error of at most 0.008.
Values may be sent and summed in bfloat16 or wider, within the bound.
A program may use at most 32 MiB of HBM per device.

v0:
```python
import jax
import jax.numpy as jnp
from jax import lax
from jax.sharding import Mesh
from jax.sharding import PartitionSpec as P

DP = ("dp_0", "dp_1")


route_scale = 2.5


def sum_by_axis(shard, axes, dim):
    for axis in axes:
        shard = lax.psum_scatter(shard, axis, scatter_dimension=dim, tiled=True)
    return shard


def in_one_piece(arrays, axis, dim, along):
    widths = [a.shape[along] for a in arrays]
    both = jnp.concatenate(arrays, axis=along)
    whole = lax.all_gather(both, axis, axis=dim, tiled=True)
    return tuple(jnp.split(whole, [sum(widths[:k]) for k in range(1, len(widths))], axis=along))


def in_one_piece_2(arrays, axis, split_dim, concat_dim, along):
    widths = [a.shape[along] for a in arrays]
    both = jnp.concatenate(arrays, axis=along)
    whole = lax.all_to_all(both, axis, split_axis=split_dim, concat_axis=concat_dim, tiled=True)
    return tuple(jnp.split(whole, [sum(widths[:k]) for k in range(1, len(widths))], axis=along))


def in_blocks(shard, dim, devices):
    before, after = (shard.shape[:dim], shard.shape[dim + 1 :])
    return jnp.moveaxis(shard.reshape(*before, devices, -1, *after), dim, 0)


def sum_at_owner(shard, axis, dim):
    devices = lax.axis_size(axis)
    parts = lax.all_to_all(in_blocks(shard, dim, devices), axis, 0, 0, tiled=True)
    return jnp.sum(parts, axis=0)


def split_pair(values):
    upper = values.astype(jnp.bfloat16)
    lower = (values - upper.astype(jnp.float32)).astype(jnp.bfloat16)
    return jnp.stack([upper, lower], axis=-1)


def join_pair(paired):
    return paired[..., 0].astype(jnp.float32) + paired[..., 1].astype(jnp.float32)


def activation_backward(hidden_grad, saved_gate, saved_up):
    gate_value = saved_gate.astype(jnp.float32)
    up_value = saved_up.astype(jnp.float32)
    gate_sigmoid = jax.nn.sigmoid(gate_value)
    activated = gate_value * gate_sigmoid
    hidden = lax.optimization_barrier((activated * up_value).astype(jnp.bfloat16)).astype(
        jnp.float32
    )
    gate_share = jnp.sum(hidden * hidden_grad, axis=1)
    gate_part = (
        hidden_grad * up_value * gate_sigmoid * (1.0 + gate_value * (1.0 - gate_sigmoid))
    ).astype(jnp.bfloat16)
    up_part = (hidden_grad * activated).astype(jnp.bfloat16)
    return (gate_part, up_part, gate_share)


def local(
    grad_output,
    router_logits,
    expert_ids,
    router_input,
    router_weight,
    gate_weight,
    up_weight,
    down_weight,
    gate_saved,
    up_saved,
):
    expert_count = lax.axis_size("expert")
    dp_count = lax.axis_size(DP)
    out_rows = grad_output[0]
    group_size, feature_share = out_rows.shape
    expert_total = router_logits.shape[2]
    top_count = expert_ids.shape[2]
    local_experts, slot_count, hidden_size = gate_saved.shape
    slot_depth = slot_count // expert_count
    assign_count = group_size * top_count
    flat_ids = expert_ids[0].reshape(assign_count)
    expert_hot = (flat_ids[:, None] == jnp.arange(expert_total, dtype=jnp.int32)[None, :]).astype(
        jnp.int32
    )
    earlier = jnp.cumsum(expert_hot, axis=0) - expert_hot
    ranking = jnp.sum(expert_hot * earlier, axis=1)
    target = flat_ids * slot_depth + ranking
    slot_place = (
        jnp.arange(expert_total * slot_depth, dtype=jnp.int32)[:, None] == target[None, :]
    ).astype(jnp.bfloat16)
    owner_hot = (
        (jnp.arange(assign_count, dtype=jnp.int32) // top_count)[:, None]
        == jnp.arange(group_size, dtype=jnp.int32)[None, :]
    ).astype(jnp.bfloat16)
    slot_token = jnp.dot(slot_place, owner_hot, preferred_element_type=jnp.float32).astype(
        jnp.bfloat16
    )
    outgoing = jnp.dot(slot_token, out_rows, preferred_element_type=jnp.float32).astype(
        jnp.bfloat16
    )
    incoming = lax.all_to_all(
        outgoing.reshape(expert_total, slot_depth, feature_share),
        "expert",
        split_axis=0,
        concat_axis=1,
        tiled=True,
    )
    partial_hidden = jnp.einsum(
        "esd,efd->esf", incoming, down_weight, preferred_element_type=jnp.float32
    )
    row_total = local_experts * slot_count
    share_rows = row_total // dp_count
    hidden_grad = sum_by_axis(partial_hidden.reshape(row_total, hidden_size), DP, 0)
    first_row = lax.axis_index(DP) * share_rows
    gate_rows = lax.dynamic_slice_in_dim(
        gate_saved.reshape(row_total, hidden_size), first_row, share_rows, 0
    )
    up_rows = lax.dynamic_slice_in_dim(
        up_saved.reshape(row_total, hidden_size), first_row, share_rows, 0
    )
    gate_part, up_part, gate_share = activation_backward(hidden_grad, gate_rows, up_rows)
    grad_gate, grad_up, gate_paired = in_one_piece(
        (gate_part, up_part, split_pair(gate_share)), DP, 0, 1
    )
    gate_grad = join_pair(gate_paired)
    grad_gate = grad_gate.reshape(local_experts, slot_count, hidden_size)
    grad_up = grad_up.reshape(local_experts, slot_count, hidden_size)
    gate_grad = gate_grad.reshape(local_experts, slot_count)
    expert_input = jnp.einsum(
        "esf,edf->esd", grad_gate, gate_weight, preferred_element_type=jnp.float32
    )
    expert_input = expert_input + jnp.einsum(
        "esf,edf->esd", grad_up, up_weight, preferred_element_type=jnp.float32
    )
    expert_input = expert_input.astype(jnp.bfloat16)
    rows_back, gate_paired_back = in_one_piece_2(
        (expert_input, split_pair(gate_grad)), "expert", 1, 0, 2
    )
    gate_back = join_pair(gate_paired_back)
    pick_map = slot_place.T.astype(jnp.float32)
    picked_gate = jnp.dot(pick_map, gate_back.reshape(expert_total * slot_depth)).reshape(
        group_size, top_count
    )
    scores = jax.nn.sigmoid(router_logits[0])
    hot_float = expert_hot.reshape(group_size, top_count, expert_total).astype(jnp.float32)
    chosen = jnp.sum(hot_float * scores[:, None, :], axis=2)
    chosen_total = jnp.sum(chosen, axis=1, keepdims=True)
    gates = route_scale * chosen / chosen_total
    mixture = jnp.sum(picked_gate * gates, axis=1, keepdims=True)
    d_chosen = (route_scale * picked_gate - mixture) / chosen_total
    d_scores = jnp.sum(hot_float * d_chosen[:, :, None], axis=1)
    logit_grad = (d_scores * scores * (1.0 - scores)).astype(jnp.bfloat16)
    grouped_input = lax.all_to_all(router_input[0], DP, split_axis=1, concat_axis=0, tiled=True)
    router_term = jnp.einsum(
        "ge,gc->ec", logit_grad, grouped_input, preferred_element_type=jnp.float32
    )
    grad_router = sum_at_owner(router_term, "expert", 0)
    picked_rows = jnp.dot(
        slot_place.T,
        rows_back.reshape(expert_total * slot_depth, feature_share),
        preferred_element_type=jnp.float32,
    )
    mixed = jnp.sum(
        gates[:, :, None] * picked_rows.reshape(group_size, top_count, feature_share), axis=1
    )
    router_part = jnp.dot(logit_grad, router_weight, preferred_element_type=jnp.float32)
    grad_input = (mixed + router_part).astype(jnp.bfloat16)[None]
    return (grad_input, grad_router)


def solution(mesh):
    torus = Mesh(mesh.devices.reshape(12, 2, mesh.shape["expert"]), ("dp_0", "dp_1", "expert"))
    placed = (
        P("expert", None, DP),
        P("expert", None, None),
        P("expert", None, None),
        P("expert", DP, None),
        P(None, DP),
        P("expert", DP, None),
        P("expert", DP, None),
        P("expert", None, DP),
        P("expert", None, None),
        P("expert", None, None),
    )
    return jax.shard_map(
        local,
        mesh=torus,
        in_specs=placed,
        out_specs=(P("expert", None, DP), P("expert", DP)),
        check_vma=False,
    )
```

profile of v0, /device:TPU:1, one launch (start us, length us, event | category | flops | bytes accessed | tf_op | source)
XLA Modules:
  0.0 318.3 jit_solution(18084469542257646535)
XLA Ops:
  7.2 0.9 copy.121
  8.3 0.1 copy.124
  8.4 0.2 fusion.20
  8.7 0.2 fusion.23
  9.0 0.6 convolution_convert_fusion
  9.6 0.2 copy.126
  9.8 0.2 reshape.239
  9.9 0.7 reshape.257
  10.6 24.3 %all_to_all.60 = bf16[32,2,1920]{2,1,0:T(2,128)(2,1)S(1)} all-to-all(bf16[32,2,1920]{2,1,0:T(2,128)(2,1)S(1)} %reshape.257), channel_id=1, replica_groups=mesh['dp_0'=12,'dp_1'=2,'expert'=32] {'expert'}, dimensions={0} | all-to-all | bytes 491520 | tf_op jit(solution)/shard_map/all_to_all | solution.py:111
  34.9 0.6 reshape.258
  35.6 0.2 copy.127
  35.7 2.2 fusion.18
  38.0 56.9 %reduce-scatter.7.cloned.1.call-done = f32[64,1024]{1,0:T(8,128)} async-done(((f32[768,1024]{1,0:T(8,128)}), f32[64,1024]{1,0:T(8,128)}) %reduce-scatter.7.cloned.1.call-update) | async-done | bytes 262160
  95.0 32.1 %reduce-scatter.9.cloned.1.call-done = f32[32,1024]{1,0:T(8,128)} async-done(((f32[64,1024]{1,0:T(8,128)}), f32[32,1024]{1,0:T(8,128)}) %reduce-scatter.9.cloned.1.call-update) | async-done | bytes 131088 | tf_op jit(solution)/shard_map/reduce_scatter | solution.py:15
  127.1 1.1 fusion.29
  128.2 1.0 multiply_reduce_fusion.1
  129.4 0.7 concatenate.6
  130.3 0.6 copy.145
  130.9 10.1 %all-to-all-start.2 = ((bf16[2,24,160]{2,0,1:T(2,128)(2,1)}), bf16[2,24,160]{2,0,1:T(2,128)(2,1)S(1)}, u32[]{:S(2)}, u32[]{:S(2)}) async-start(bf16[2,24,160]{2,0,1:T(2,128)(2,1)} %copy.145), calls=%async_computation.2 | async-start | bytes 49152 | tf_op jit(solution)/shard_map/all_to_all | solution.py:163
  141.1 115.9 %all-gather.2.cloned.1.call-done = bf16[768,2050]{1,0:T(8,128)(2,1)} async-done(((bf16[32,2050]{1,0:T(8,128)(2,1)}), bf16[768,2050]{1,0:T(8,128)(2,1)}) %all-gather.2.cloned.1.call-update) | async-done | bytes 3148816 | tf_op jit(solution)/shard_map/all_gather | solution.py:22
  257.0 1.3 add_reduce_fusion
  258.4 2.3 fusion.44
  260.7 0.7 fusion.47
  261.4 0.6 copy-done.2
  262.0 0.7 fusion
  262.8 1.0 copy.137
  263.8 14.3 %all-to-all-start.1 = ((bf16[4,192,162]{2,0,1:T(4,128)(2,1)}), bf16[4,192,162]{2,0,1:T(4,128)(2,1)S(1)}, u32[]{:S(2)}, u32[]{:S(2)}) async-start(bf16[4,192,162]{2,0,1:T(4,128)(2,1)} %copy.137), calls=%async_computation.1 | async-start | bytes 786432 | tf_op jit(solution)/shard_map/all_to_all | solution.py:29
  278.2 0.8 fusion.24
  279.0 12.9 %all-to-all-done.1 = bf16[4,192,162]{2,0,1:T(4,128)(2,1)S(1)} async-done(((bf16[4,192,162]{2,0,1:T(4,128)(2,1)}), bf16[4,192,162]{2,0,1:T(4,128)(2,1)S(1)}, u32[]{:S(2)}, u32[]{:S(2)}) %all-to-all-start.1) | async-done | bytes 248864 | tf_op jit(solution)/shard_map/all_to_all | solution.py:29
  291.9 0.1 copy.138
  292.0 0.2 all_to_all.50
  292.3 0.2 fusion.45
  292.5 0.2 copy.139
  292.7 0.2 reshape.245
  293.1 0.1 copy.155
  293.2 0.1 copy.143
  293.4 0.2 reshape.247
  293.5 1.5 fusion.5
  295.0 0.2 multiply_reduce_fusion.2
  295.3 0.2 multiply_reduce_fusion
  295.5 0.1 copy.144
  295.6 0.1 fusion.37
  295.7 0.7 copy.147
  296.5 5.2 %all-to-all-start.3 = ((f32[32,4,160]{2,1,0:T(4,128)}), f32[32,4,160]{2,1,0:T(4,128)S(1)}, u32[]{:S(2)}, u32[]{:S(2)}) async-start(f32[32,4,160]{2,1,0:T(4,128)} %copy.147), calls=%async_computation.3 | async-start | bytes 262144 | tf_op jit(solution)/shard_map/all_to_all | solution.py:40
  301.7 0.4 fusion.7
  302.1 0.8 fusion.12
  302.9 8.2 %all-to-all-done.3 = f32[32,4,160]{2,1,0:T(4,128)S(1)} async-done(((f32[32,4,160]{2,1,0:T(4,128)}), f32[32,4,160]{2,1,0:T(4,128)S(1)}, u32[]{:S(2)}, u32[]{:S(2)}) %all-to-all-start.3) | async-done | bytes 81952 | tf_op jit(solution)/shard_map/all_to_all | solution.py:40
  311.1 0.6 reduce_sum.85
  (43 shorter events, 1.4 us)
Async XLA Ops:
  7.2 28.6 %copy-start = (bf16[4,1024,160]{1,2,0:T(8,128)(2,1)S(1)}, bf16[4,1024,160]{1,2,0:T(8,128)(2,1)}, u32[]{:S(2)}) copy-start(bf16[4,1024,160]{1,2,0:T(8,128)(2,1)} %param.17) | copy-start | bytes 3932164
  7.2 1.8 copy-start.6
  7.2 87.7 %reduce-scatter.7.cloned.1.call-start = ((), (), s32[]{:S(2)}) async-start(), calls=%async_computation.7 | async-start | bytes 3407872
  38.0 92.2 %copy-start.5 = (bf16[1,2,3840]{2,1,0:T(2,128)(2,1)S(1)}, bf16[1,2,3840]{2,1,0:T(2,128)(2,1)}, u32[]{:S(2)}) copy-start(bf16[1,2,3840]{2,1,0:T(2,128)(2,1)} %param.13) | copy-start | bytes 46084
  38.0 89.1 %reduce-scatter.9.cloned.1.call-start = ((), (), s32[]{:S(2)}) async-start(), calls=%async_computation.8 | async-start | bytes 393216 | tf_op jit(solution)/shard_map/reduce_scatter | solution.py:15
  94.9 162.1 %all-gather.2.cloned.1.call-start = ((), (), s32[]{:S(2)}) async-start(), calls=%async_computation.6 | async-start | bytes 3481600 | tf_op jit(solution)/shard_map/all_gather | solution.py:22
  130.9 132.9 %all-to-all-start.2 = ((bf16[2,24,160]{2,0,1:T(2,128)(2,1)}), bf16[2,24,160]{2,0,1:T(2,128)(2,1)S(1)}, u32[]{:S(2)}, u32[]{:S(2)}) async-start(bf16[2,24,160]{2,0,1:T(2,128)(2,1)} %copy.145), calls=%async_computation.2 | async-start | bytes 49152 | tf_op jit(solution)/shard_map/all_to_all | solution.py:163
  258.4 2.3 copy-start.1
  260.7 1.3 copy-start.2
  262.7 15.4 %copy-start.3 = (f32[1,48,128]{2,1,0:T(8,128)S(1)}, f32[1,48,128]{2,1,0:T(8,128)}, u32[]{:S(2)}) copy-start(f32[1,48,128]{2,1,0:T(8,128)} %param.11) | copy-start | bytes 73732
  263.8 28.1 %all-to-all-start.1 = ((bf16[4,192,162]{2,0,1:T(4,128)(2,1)}), bf16[4,192,162]{2,0,1:T(4,128)(2,1)S(1)}, u32[]{:S(2)}, u32[]{:S(2)}) async-start(bf16[4,192,162]{2,0,1:T(4,128)(2,1)} %copy.137), calls=%async_computation.1 | async-start | bytes 786432 | tf_op jit(solution)/shard_map/all_to_all | solution.py:29
  293.0 9.0 %copy-start.4 = (bf16[128,160]{0,1:T(8,128)(2,1)S(1)}, bf16[128,160]{0,1:T(8,128)(2,1)}, u32[]{:S(2)}) copy-start(bf16[128,160]{0,1:T(8,128)(2,1)} %param.14) | copy-start | bytes 122884
  296.5 14.6 %all-to-all-start.3 = ((f32[32,4,160]{2,1,0:T(4,128)}), f32[32,4,160]{2,1,0:T(4,128)S(1)}, u32[]{:S(2)}, u32[]{:S(2)}) async-start(f32[32,4,160]{2,1,0:T(4,128)} %copy.147), calls=%async_computation.3 | async-start | bytes 262144 | tf_op jit(solution)/shard_map/all_to_all | solution.py:40
Sparse Core Ops, SparseCore 0:
  38.1 56.7 reduce-scatter.6
  98.0 29.0 reduce-scatter.8
  130.7 126.2 all-gather.1
where the time goes:
time: 319 us; the launch traced here: 318 us
  waiting for transfers between devices  226 us (71%)
  starting transfers between devices  29.8 us (9%)
  blocking collectives  24.3 us (8%)
  between operations  14.1 us (4%)
  local copies, waits for them, and re-layouts  11.2 us (4%)
  matrix products  7.01 us (2%)
  other arithmetic  5.91 us (2%)
    all_gather x1, waiting for transfers between devices, in_one_piece(): whole = lax.all_gather(both, axis, axis=dim, tiled=True)  116 us
    unnamed x4, waiting for transfers between devices  56.9 us
    reduce_scatter x1, waiting for transfers between devices, sum_by_axis(): shard = lax.psum_scatter(shard, axis, scatter_dimension=dim, tiled=True)  32.1 us
    all_to_all x1, blocking collectives, local(): lax.all_to_all(outgoing.reshape(expert_total, slot_depth, feature_share),...  24.3 us
    all_to_all x1, starting transfers between devices, in_one_piece_2(): lax.all_to_all(both, axis, split_axis=split_dim, concat_axis=concat_dim,...  14.3 us
    all_to_all x1, waiting for transfers between devices, in_one_piece_2(): lax.all_to_all(both, axis, split_axis=split_dim, concat_axis=concat_dim,...  12.9 us
    all_to_all x1, starting transfers between devices, local(): lax.all_to_all(router_input[0], DP, split_axis=1, concat_axis=0, tiled=True)  10.1 us
    all_to_all x1, waiting for transfers between devices, sum_at_owner(): lax.all_to_all(in_blocks(shard, dim, devices), axis, 0, 0, tiled=True)  8.25 us
  transfers between devices with their start and end apart: 6, of which 5 were waited for; matrix products, arithmetic and copies ran while one was open for 3% of the time, Pallas kernels for 0%

commit v1 on v0

v1 whole, which is shorter than its diff:
```python
import functools

import jax
import jax.numpy as jnp
from jax import lax
from jax.experimental import pallas as pl
from jax.experimental.pallas import tpu as pltpu
from jax.sharding import Mesh
from jax.sharding import PartitionSpec as P

DP = ("dp_0", "dp_1")
MESH = pl.DeviceIdType.MESH
VMEM = pl.BlockSpec(memory_space=pltpu.VMEM)

route_scale = 2.5


def greet(peers):
    barrier = pltpu.get_barrier_semaphore()
    for peer in peers:
        pl.semaphore_signal(barrier, inc=1, device_id=peer, device_id_type=MESH)
    pl.semaphore_wait(barrier, len(peers))


def exchange_start(axis, count, src_ref, dst_ref, send_sem, recv_sem):
    me = lax.axis_index(axis)

    def start(k, carry):
        peer = lax.rem(me + k, count)
        pltpu.make_async_remote_copy(
            src_ref=src_ref.at[peer],
            dst_ref=dst_ref.at[me],
            send_sem=send_sem.at[k],
            recv_sem=recv_sem.at[k],
            device_id={axis: peer},
            device_id_type=MESH,
        ).start()
        return carry

    lax.fori_loop(1, count, start, 0)
    dst_ref[me] = src_ref[me]


def exchange_wait(axis, count, src_ref, dst_ref, send_sem, recv_sem):
    me = lax.axis_index(axis)

    def wait(k, carry):
        peer = lax.rem(me + k, count)
        pltpu.make_async_remote_copy(
            src_ref=src_ref.at[peer],
            dst_ref=dst_ref.at[me],
            send_sem=send_sem.at[k],
            recv_sem=recv_sem.at[k],
            device_id={axis: peer},
            device_id_type=MESH,
        ).wait()
        return carry

    lax.fori_loop(1, count, wait, 0)


def exchange_kernel(count, src_ref, dst_ref, send_sem, recv_sem):
    me = lax.axis_index("expert")
    barrier = pltpu.get_barrier_semaphore()

    def signal(k, carry):
        pl.semaphore_signal(
            barrier, inc=1, device_id={"expert": lax.rem(me + k, count)}, device_id_type=MESH
        )
        return carry

    lax.fori_loop(1, count, signal, 0)
    pl.semaphore_wait(barrier, count - 1)
    exchange_start("expert", count, src_ref, dst_ref, send_sem, recv_sem)
    exchange_wait("expert", count, src_ref, dst_ref, send_sem, recv_sem)


def exchange(blocks, collective_id):
    count = blocks.shape[0]
    return pl.pallas_call(
        functools.partial(exchange_kernel, count),
        out_shape=jax.ShapeDtypeStruct(blocks.shape, blocks.dtype),
        in_specs=[VMEM],
        out_specs=VMEM,
        scratch_shapes=[pltpu.SemaphoreType.DMA((count,)), pltpu.SemaphoreType.DMA((count,))],
        compiler_params=pltpu.CompilerParams(
            collective_id=collective_id, has_side_effects=True
        ),
    )(blocks)


def dispatch_kernel(
    count, dp_0, dp_1, src_ref, row_ref, dst_ref, got_ref, send_sem, recv_sem, row_send, row_recv
):
    me = lax.axis_index("expert")
    z, h = lax.axis_index("dp_0"), lax.axis_index("dp_1")
    dp_count = dp_0 * dp_1
    mine = z * dp_1 + h
    barrier = pltpu.get_barrier_semaphore()

    def signal(k, carry):
        pl.semaphore_signal(
            barrier, inc=1, device_id={"expert": lax.rem(me + k, count)}, device_id_type=MESH
        )
        return carry

    def signal_dp(k, carry):
        peer = lax.rem(mine + k, dp_count)
        pl.semaphore_signal(
            barrier,
            inc=1,
            device_id={"dp_0": peer // dp_1, "dp_1": lax.rem(peer, dp_1)},
            device_id_type=MESH,
        )
        return carry

    def row_copy(k):
        peer = lax.rem(mine + k, dp_count)
        return pltpu.make_async_remote_copy(
            src_ref=row_ref.at[peer],
            dst_ref=got_ref.at[mine],
            send_sem=row_send.at[k],
            recv_sem=row_recv.at[k],
            device_id={"dp_0": peer // dp_1, "dp_1": lax.rem(peer, dp_1)},
            device_id_type=MESH,
        )

    def start_row(k, carry):
        row_copy(k).start()
        return carry

    def wait_row(k, carry):
        row_copy(k).wait()
        return carry

    lax.fori_loop(1, dp_count, signal_dp, 0)
    lax.fori_loop(1, count, signal, 0)
    pl.semaphore_wait(barrier, count - 1 + dp_count - 1)
    lax.fori_loop(1, dp_count, start_row, 0)
    exchange_start("expert", count, src_ref, dst_ref, send_sem, recv_sem)
    got_ref[mine] = row_ref[mine]
    exchange_wait("expert", count, src_ref, dst_ref, send_sem, recv_sem)
    lax.fori_loop(1, dp_count, wait_row, 0)


def dispatch(blocks, rows, dp_0, dp_1, collective_id):
    count, dp_count = blocks.shape[0], rows.shape[0]
    return pl.pallas_call(
        functools.partial(dispatch_kernel, count, dp_0, dp_1),
        out_shape=(
            jax.ShapeDtypeStruct(blocks.shape, blocks.dtype),
            jax.ShapeDtypeStruct(rows.shape, rows.dtype),
        ),
        in_specs=[VMEM, VMEM],
        out_specs=(VMEM, VMEM),
        scratch_shapes=[
            pltpu.SemaphoreType.DMA((count,)),
            pltpu.SemaphoreType.DMA((count,)),
            pltpu.SemaphoreType.DMA((dp_count,)),
            pltpu.SemaphoreType.DMA((dp_count,)),
        ],
        compiler_params=pltpu.CompilerParams(
            collective_id=collective_id, has_side_effects=True
        ),
    )(blocks, rows)


def all_sum_kernel(
    ring, parts, own_ref, out_ref, send_buf, recv_buf, swap_buf, send_sem, recv_sem, swap_send, swap_recv, gsend, grecv
):
    z, h = lax.axis_index("dp_0"), lax.axis_index("dp_1")
    half = ring // 2
    rows = own_ref.shape[1] // parts
    neighbour = ({"dp_0": lax.rem(z + 1, ring)}, {"dp_0": lax.rem(z + ring - 1, ring)})
    partner = {"dp_1": 1 - h}
    greet((*neighbour, partner))

    def at(way, distance):
        step = distance if way == 0 else ring - distance
        return lax.rem(z + step, ring)

    def piece(g):
        return pl.ds(g * rows, rows)

    def runs(way, distance, g):
        if distance < half or ring % 2:
            return True
        return (g < parts // 2) == (way == 0)

    def hop(way, step, g):
        return pltpu.make_async_remote_copy(
            src_ref=send_buf.at[way, step, piece(g)],
            dst_ref=recv_buf.at[way, step, piece(g)],
            send_sem=send_sem.at[way, step, g],
            recv_sem=recv_sem.at[way, step, g],
            device_id=neighbour[way],
            device_id_type=MESH,
        )

    def swap(g):
        return pltpu.make_async_remote_copy(
            src_ref=swap_buf.at[0, piece(g)],
            dst_ref=swap_buf.at[1, piece(g)],
            send_sem=swap_send.at[g],
            recv_sem=swap_recv.at[g],
            device_id=partner,
            device_id_type=MESH,
        )

    def gather(way, step, g):
        block = at(1 - way, step) if step else z
        return pltpu.make_async_remote_copy(
            src_ref=out_ref.at[block, piece(g)],
            dst_ref=out_ref.at[block, piece(g)],
            send_sem=gsend.at[way, step, g],
            recv_sem=grecv.at[way, step, g],
            device_id=neighbour[way],
            device_id_type=MESH,
        )

    for step in range(half):
        distance = half - step
        for g in range(parts):
            for way in range(2):
                if not runs(way, distance, g):
                    continue
                value = own_ref[at(way, distance), piece(g), :]
                if step and runs(way, distance + 1, g):
                    hop(way, step - 1, g).wait_recv()
                    value = value + recv_buf[way, step - 1, piece(g), :].astype(jnp.float32)
                send_buf[way, step, piece(g), :] = value.astype(jnp.bfloat16)
                hop(way, step, g).start()
    for g in range(parts):
        value = own_ref[z, piece(g), :]
        for way in range(2):
            hop(way, half - 1, g).wait_recv()
            value = value + recv_buf[way, half - 1, piece(g), :].astype(jnp.float32)
        swap_buf[0, piece(g), :] = value.astype(jnp.bfloat16)
        swap(g).start()
    for g in range(parts):
        swap(g).wait_recv()
        total = swap_buf[0, piece(g), :].astype(jnp.float32) + swap_buf[1, piece(g), :].astype(
            jnp.float32
        )
        out_ref[z, piece(g), :] = total.astype(jnp.bfloat16)
        for way in range(2):
            gather(way, 0, g).start()
    for step in range(1, half):
        for g in range(parts):
            for way in range(2):
                gather(way, step - 1, g).wait_recv()
                if runs(way, step + 1, g):
                    gather(way, step, g).start()
    for g in range(parts):
        for way in range(2):
            if runs(way, half, g):
                gather(way, half - 1, g).wait_recv()
    for step in range(half):
        for g in range(parts):
            for way in range(2):
                if runs(way, half - step, g):
                    hop(way, step, g).wait_send()
                if runs(way, step + 1, g):
                    gather(way, step, g).wait_send()
    for g in range(parts):
        swap(g).wait_send()


def all_sum(partial, ring, parts, collective_id):
    row_total, width = partial.shape
    depth = row_total // ring
    half = ring // 2
    sems = pltpu.SemaphoreType.DMA((2, half, parts))
    total = pl.pallas_call(
        functools.partial(all_sum_kernel, ring, parts),
        out_shape=jax.ShapeDtypeStruct((ring, depth, width), jnp.bfloat16),
        in_specs=[VMEM],
        out_specs=VMEM,
        scratch_shapes=[
            pltpu.VMEM((2, half, depth, width), jnp.bfloat16),
            pltpu.VMEM((2, half, depth, width), jnp.bfloat16),
            pltpu.VMEM((2, depth, width), jnp.bfloat16),
            sems,
            sems,
            pltpu.SemaphoreType.DMA((parts,)),
            pltpu.SemaphoreType.DMA((parts,)),
            sems,
            sems,
        ],
        compiler_params=pltpu.CompilerParams(
            collective_id=collective_id, has_side_effects=True
        ),
    )(partial.reshape(ring, depth, width))
    return total.reshape(row_total, width)


def split_pair(values):
    upper = values.astype(jnp.bfloat16)
    lower = (values - upper.astype(jnp.float32)).astype(jnp.bfloat16)
    return upper, lower


def activation_backward(hidden_grad, saved_gate, saved_up):
    gate_value = saved_gate.astype(jnp.float32)
    up_value = saved_up.astype(jnp.float32)
    gate_sigmoid = jax.nn.sigmoid(gate_value)
    activated = gate_value * gate_sigmoid
    hidden = (activated * up_value).astype(jnp.bfloat16).astype(jnp.float32)
    gate_share = jnp.sum(hidden * hidden_grad, axis=1)
    gate_part = (
        hidden_grad * up_value * gate_sigmoid * (1.0 + gate_value * (1.0 - gate_sigmoid))
    ).astype(jnp.bfloat16)
    up_part = (hidden_grad * activated).astype(jnp.bfloat16)
    return (gate_part, up_part, gate_share)


def local(
    grad_output,
    router_logits,
    expert_ids,
    router_input,
    router_weight,
    gate_weight,
    up_weight,
    down_weight,
    gate_saved,
    up_saved,
):
    expert_count = lax.axis_size("expert")
    dp_0, dp_1 = lax.axis_size("dp_0"), lax.axis_size("dp_1")
    dp_count = dp_0 * dp_1
    out_rows = grad_output[0]
    group_size, feature_share = out_rows.shape
    expert_total = router_logits.shape[2]
    top_count = expert_ids.shape[2]
    local_experts, slot_count, hidden_size = gate_saved.shape
    slot_depth = slot_count // expert_count
    block_rows = local_experts * slot_depth
    block_lanes = block_rows * feature_share // 128
    assign_count = group_size * top_count
    flat_ids = expert_ids[0].reshape(assign_count)
    expert_hot = (flat_ids[:, None] == jnp.arange(expert_total, dtype=jnp.int32)[None, :]).astype(
        jnp.int32
    )
    earlier = jnp.cumsum(expert_hot, axis=0) - expert_hot
    ranking = jnp.sum(expert_hot * earlier, axis=1)
    target = flat_ids * slot_depth + ranking
    slot_place = (
        jnp.arange(expert_total * slot_depth, dtype=jnp.int32)[:, None] == target[None, :]
    ).astype(jnp.bfloat16)
    owner_hot = (
        (jnp.arange(assign_count, dtype=jnp.int32) // top_count)[:, None]
        == jnp.arange(group_size, dtype=jnp.int32)[None, :]
    ).astype(jnp.bfloat16)
    slot_token = jnp.dot(slot_place, owner_hot, preferred_element_type=jnp.float32).astype(
        jnp.bfloat16
    )
    outgoing = jnp.dot(slot_token, out_rows, preferred_element_type=jnp.float32).astype(
        jnp.bfloat16
    )
    blocks = outgoing.reshape(expert_count, block_lanes, 128)
    share_pad = -feature_share % 128
    router_rows = jnp.pad(
        jnp.swapaxes(router_input[0].reshape(-1, dp_count, feature_share), 0, 1),
        ((0, 0), (0, 0), (0, share_pad)),
    )
    incoming, grouped = dispatch(blocks, router_rows, dp_0, dp_1, 0)
    incoming = jnp.swapaxes(
        incoming.reshape(expert_count, local_experts, slot_depth, feature_share), 0, 1
    ).reshape(local_experts, slot_count, feature_share)
    grouped_input = grouped[:, :, :feature_share].reshape(group_size, feature_share)
    partial_hidden = jnp.einsum(
        "esd,efd->esf", incoming, down_weight, preferred_element_type=jnp.float32
    )
    row_total = local_experts * slot_count
    hidden_grad = all_sum(partial_hidden.reshape(row_total, hidden_size), dp_0, 2, 1)
    grad_gate, grad_up, gate_grad = activation_backward(
        hidden_grad.astype(jnp.float32),
        gate_saved.reshape(row_total, hidden_size),
        up_saved.reshape(row_total, hidden_size),
    )
    grad_gate = grad_gate.reshape(local_experts, slot_count, hidden_size)
    grad_up = grad_up.reshape(local_experts, slot_count, hidden_size)
    expert_input = jnp.einsum(
        "esf,edf->esd", grad_gate, gate_weight, preferred_element_type=jnp.float32
    )
    expert_input = expert_input + jnp.einsum(
        "esf,edf->esd", grad_up, up_weight, preferred_element_type=jnp.float32
    )
    expert_input = expert_input.astype(jnp.bfloat16)

    def by_group(values):
        split = values.reshape(local_experts, expert_count, slot_depth, *values.shape[2:])
        return jnp.swapaxes(split, 0, 1)

    upper, lower = split_pair(by_group(gate_grad.reshape(local_experts, slot_count)))
    gate_rows = jnp.pad(
        jnp.stack([upper, lower], axis=1).reshape(expert_count, 2, block_rows),
        ((0, 0), (0, 0), (0, 128 - block_rows)),
    )
    returning = jnp.concatenate(
        [by_group(expert_input).reshape(expert_count, block_lanes, 128), gate_rows], axis=1
    )
    returned = exchange(returning, 2)
    rows_back = returned[:, :block_lanes].reshape(expert_total * slot_depth, feature_share)
    gate_back = (
        returned[:, block_lanes, :block_rows].astype(jnp.float32)
        + returned[:, block_lanes + 1, :block_rows].astype(jnp.float32)
    ).reshape(expert_total * slot_depth, 1)
    picked_gate = jnp.sum(
        jnp.where(
            jnp.arange(expert_total * slot_depth, dtype=jnp.int32)[:, None] == target[None, :],
            gate_back,
            0.0,
        ),
        axis=0,
    ).reshape(group_size, top_count)
    scores = jax.nn.sigmoid(router_logits[0])
    hot_float = expert_hot.reshape(group_size, top_count, expert_total).astype(jnp.float32)
    chosen = jnp.sum(hot_float * scores[:, None, :], axis=2)
    chosen_total = jnp.sum(chosen, axis=1, keepdims=True)
    gates = route_scale * chosen / chosen_total
    mixture = jnp.sum(picked_gate * gates, axis=1, keepdims=True)
    d_chosen = (route_scale * picked_gate - mixture) / chosen_total
    d_scores = jnp.sum(hot_float * d_chosen[:, :, None], axis=1)
    logit_grad = (d_scores * scores * (1.0 - scores)).astype(jnp.bfloat16)
    router_term = jnp.einsum(
        "ge,gc->ec", logit_grad, grouped_input, preferred_element_type=jnp.float32
    )
    term_blocks = router_term.reshape(expert_count, local_experts * feature_share // 128, 128)
    grad_router = jnp.sum(exchange(term_blocks, 3), axis=0).reshape(local_experts, feature_share)
    picked_rows = jnp.dot(
        slot_place.T, rows_back, preferred_element_type=jnp.float32
    )
    mixed = jnp.sum(
        gates[:, :, None] * picked_rows.reshape(group_size, top_count, feature_share), axis=1
    )
    router_part = jnp.dot(logit_grad, router_weight, preferred_element_type=jnp.float32)
    grad_input = (mixed + router_part).astype(jnp.bfloat16)[None]
    return (grad_input, grad_router)


def solution(mesh):
    torus = Mesh(
        mesh.devices.reshape(mesh.shape["dp"] // 2, 2, mesh.shape["expert"]),
        ("dp_0", "dp_1", "expert"),
    )
    placed = (
        P("expert", None, DP),
        P("expert", None, None),
        P("expert", None, None),
        P("expert", DP, None),
        P(None, DP),
        P("expert", DP, None),
        P("expert", DP, None),
        P("expert", None, DP),
        P("expert", None, None),
        P("expert", None, None),
    )
    return jax.shard_map(
        local,
        mesh=torus,
        in_specs=placed,
        out_specs=(P("expert", None, DP), P("expert", DP)),
        check_vma=False,
    )
```

time: 319 us -> 147 us (0.46)
  waiting for transfers between devices: 226 us -> 0 us
  Pallas kernels: 0 us -> 118 us
  starting transfers between devices: 29.8 us -> 0 us
  blocking collectives: 24.3 us -> 0 us
  between operations: 14.1 us -> 1.02 us
  other arithmetic: 5.91 us -> 11.1 us
    pallas_call x0 -> x4, Pallas kernels: none -> 118 us  [the longest x1 48.2 us: all_sum(): pl.pallas_call(functools.partial(all_sum_kernel, ring, parts), out_shape=...]
    all_gather x1 -> x0, waiting for transfers between devices: 116 us -> none  [in_one_piece(): whole = lax.all_gather(both, axis, axis=dim, tiled=True)]
    unnamed x4 -> x0, waiting for transfers between devices: 56.9 us -> none
    reduce_scatter x1 -> x0, waiting for transfers between devices: 32.1 us -> none  [sum_by_axis(): shard = lax.psum_scatter(shard, axis, scatter_dimension=dim, tiled=True)]
    all_to_all x3 -> x0, starting transfers between devices: 29.7 us -> none  [the longest x1 14.3 us: in_one_piece_2(): lax.all_to_all(both, axis, split_axis=split_dim, concat_axis=concat_dim,...]
    all_to_all x1 -> x0, blocking collectives: 24.3 us -> none  [local(): lax.all_to_all(outgoing.reshape(expert_total, slot_depth, feature_share),...]
    all_to_all x3 -> x0, waiting for transfers between devices: 21.1 us -> none  [the longest x1 12.9 us: in_one_piece_2(): lax.all_to_all(both, axis, split_axis=split_dim, concat_axis=concat_dim,...]
    convert_element_type x4 -> x1, other arithmetic: 1.09 us -> 6.31 us  [activation_backward(): gate_part = (hidden_grad * up_value * gate_sigmoid * (1.0 + gate_value *...]
  transfers between devices with their start and end apart: 6 -> 0, of which waited for: 5 -> 0; matrix products, arithmetic and copies ran while one was open for 3% -> 0% of each run, Pallas kernels for 0% -> 0%
where the time goes in v1:
time: 147 us
  Pallas kernels  118 us (80%)
  other arithmetic  11.1 us (8%)
  local copies, waits for them, and re-layouts  8.57 us (6%)
  matrix products  7.98 us (5%)
    pallas_call x1, Pallas kernels, all_sum(): pl.pallas_call(functools.partial(all_sum_kernel, ring, parts), out_shape=...  48.2 us
    pallas_call x2, Pallas kernels, exchange(): pl.pallas_call(functools.partial(exchange_kernel, count), out_shape=jax.S...  38.3 us
    pallas_call x1, Pallas kernels, dispatch(): pl.pallas_call(functools.partial(dispatch_kernel, count, dp_0, dp_1), out...  31.8 us
    convert_element_type x1, other arithmetic, activation_backward(): gate_part = (hidden_grad * up_value * gate_sigmoid * (1.0 + gate_value *...  6.31 us
    dot_general x1, matrix products, local(): jnp.einsum('esf,edf->esd', grad_up, up_weight, preferred_element_type=jnp...  3.05 us

profile of v1, /device:TPU:1, one launch (start us, length us, event | category | flops | bytes accessed | tf_op | source)
XLA Modules:
  0.0 146.9 jit_solution(10219006128817024408)
XLA Ops:
  0.6 0.0 copy-start
  0.7 0.9 copy.53
  1.5 0.1 eq.88
  1.6 0.1 copy.55
  1.7 0.2 fusion.28
  2.0 0.1 broadcast_add_fusion
  2.1 0.1 reshape_squeeze.6
  2.2 0.2 fusion.31
  2.4 0.6 convolution_convert_fusion
  3.1 0.2 copy.57
  3.2 1.2 reshape.210.src_ref
  4.5 0.1 reshape_squeeze.7
  4.6 0.6 pad.8.row_ref
  5.3 31.8 %shard_map.113 = (bf16[32,30,128]{2,1,0:T(8,128)(2,1)}, bf16[24,2,256]{2,1,0:T(2,128)(2,1)}) custom-call(bf16[32,30,128]{2,1,0:T(8,128)(2,1)} %reshape.210.src_ref, bf16[24,2,256]{2,1,0:T(2,128)(2,1)} %pad.8.row_ref), custom_call_target="tpu_custom_call" | custom-call | tf_op jit(solution)/shard_map/pallas_call | solution.py:148
  37.1 1.5 %reshape.211 = bf16[32,4,6,160]{3,2,1,0:T(8,128)(2,1)S(1)} reshape(bf16[32,30,128]{2,1,0:T(8,128)(2,1)} %get-tuple-element.4) | data formatting | bytes 491520 | tf_op jit(solution)/shard_map/reshape | solution.py:369
  38.6 0.2 copy.59
  38.8 2.2 %fusion.26 = f32[4,192,1024]{2,1,0:T(8,128)} fusion(bf16[4,1024,160]{1,2,0:T(8,128)(2,1)S(1)} %copy-done, bf16[4,192,160]{2,0,1:T(4,128)(2,1)S(1)} %bitcast.78), kind=kOutput, calls=%fused_computation.35 | convolution fusion | flops 251658240 | bytes 4702208 | tf_op jit(solution)/shard_map/esd,efd->esf/dot_general | solution.py:372
  41.0 48.2 %shard_map.114 = bf16[12,64,1024]{2,1,0:T(8,128)(2,1)} custom-call(f32[12,64,1024]{2,1,0:T(8,128)} %bitcast.74), custom_call_target="tpu_custom_call" | custom-call | tf_op jit(solution)/shard_map/pallas_call | solution.py:274
  89.2 6.3 %fusion.6 = (bf16[4,192,1024]{2,1,0:T(8,128)(2,1)}, f32[4,192]{1,0:T(4,128)S(1)}) fusion(bf16[4,192,1024]{2,1,0:T(8,128)(2,1)} %param.18, bf16[4,192,1024]{2,1,0:T(8,128)(2,1)} %param.19, bf16[4,192,1024]{2,1,0:T(8,128)(2,1)} %bitcast.75), kind=kLoop, calls=%fused_computation.13 | loop fusion | flops 14941440 | bytes 6294528 | tf_op jit(solution)/shard_map/convert_element_type | solution.py:312
  95.5 0.1 reshape_reshape.7
  95.6 0.1 copy.63
  95.8 0.1 copy.66
  95.9 0.1 copy.67
  96.0 0.1 fusion.42
  96.1 3.1 %fusion.10 = f32[4,192,160]{1,2,0:T(8,128)S(1)} fusion(bf16[4,160,1024]{2,1,0:T(8,128)(2,1)} %param.16, bf16[4,192,1024]{2,1,0:T(8,128)(2,1)S(1)} %bitcast.76, bf16[4,192,1024]{2,1,0:T(8,128)(2,1)} %param.18), kind=kOutput, calls=%fused_computation.17 | convolution fusion | flops 257949696 | bytes 4947968 | tf_op jit(solution)/shard_map/esf,edf->esd/dot_general | solution.py:387
  99.2 0.7 fusion.12
  99.9 0.3 copy.61
  100.2 0.1 copy.62
  100.3 0.5 reshape.214
  100.8 0.8 pad_maximum_fusion.src_ref
  101.5 25.7 %shard_map.115 = bf16[32,32,128]{2,1,0:T(8,128)(2,1)} custom-call(bf16[32,32,128]{2,1,0:T(8,128)(2,1)} %pad_maximum_fusion.src_ref), custom_call_target="tpu_custom_call" | custom-call | tf_op jit(solution)/shard_map/pallas_call | solution.py:80
  127.3 1.1 add_reduce_fusion
  128.3 0.1 add.57
  128.4 0.2 select_reduce_fusion
  128.6 0.1 reshape.216
  128.7 0.1 copy.52
  128.8 0.8 fusion.32
  129.6 0.2 multiply_reduce_fusion.1
  129.8 0.1 subtract_divide_fusion
  129.9 0.2 multiply_reduce_fusion
  130.1 0.2 fusion.44
  130.3 0.8 reshape.218.src_ref
  131.1 12.6 %shard_map.116 = f32[32,5,128]{2,1,0:T(8,128)} custom-call(f32[32,5,128]{2,1,0:T(8,128)} %reshape.218.src_ref), custom_call_target="tpu_custom_call" | custom-call | tf_op jit(solution)/shard_map/pallas_call | solution.py:80
  143.7 0.9 reduce_sum.92
  144.6 0.7 reshape.219
  145.3 0.4 reshape.215
  145.7 0.4 fusion.16
  146.1 0.8 fusion.21
  (33 shorter events, 0.2 us)
Async XLA Ops:
  0.6 38.1 %copy-start = (bf16[4,1024,160]{1,2,0:T(8,128)(2,1)S(1)}, bf16[4,1024,160]{1,2,0:T(8,128)(2,1)}, u32[]{:S(2)}) copy-start(bf16[4,1024,160]{1,2,0:T(8,128)(2,1)} %param.17) | copy-start | bytes 3932164
  0.6 1.8 %copy-start.10 = (bf16[1,48,160]{2,1,0:T(8,128)(2,1)S(1)}, bf16[1,48,160]{2,1,0:T(8,128)(2,1)}, u32[]{:S(2)}) copy-start(bf16[1,48,160]{2,1,0:T(8,128)(2,1)} %param.10) | copy-start | bytes 46084
  1.9 2.5 %copy-start.9 = (bf16[1,2,3840]{2,1,0:T(2,128)(2,1)S(1)}, bf16[1,2,3840]{2,1,0:T(2,128)(2,1)}, u32[]{:S(2)}) copy-start(bf16[1,2,3840]{2,1,0:T(2,128)(2,1)} %param.13) | copy-start | bytes 46084
  89.2 6.9 %copy-start.1 = (bf16[12,64,1024]{2,1,0:T(8,128)(2,1)S(1)}, bf16[12,64,1024]{2,1,0:T(8,128)(2,1)}, u32[]{:S(2)}) copy-start(bf16[12,64,1024]{2,1,0:T(8,128)(2,1)} %shard_map.114) | copy-start | bytes 4718596
  96.1 3.1 %copy-start.2 = (bf16[4,192,1024]{2,1,0:T(8,128)(2,1)S(1)}, bf16[4,192,1024]{2,1,0:T(8,128)(2,1)}, u32[]{:S(2)}) copy-start(bf16[4,192,1024]{2,1,0:T(8,128)(2,1)} %get-tuple-element.12) | copy-start | bytes 4718596
  96.1 3.1 %copy-start.3 = (bf16[4,160,1024]{2,1,0:T(8,128)(2,1)S(1)}, bf16[4,160,1024]{2,1,0:T(8,128)(2,1)}, u32[]{:S(2)}) copy-start(bf16[4,160,1024]{2,1,0:T(8,128)(2,1)} %param.15) | copy-start | bytes 3932164
  100.1 28.6 %copy-start.8 = (s32[1,48,8]{1,2,0:T(8,128)S(1)}, s32[1,48,8]{1,2,0:T(8,128)}, u32[]{:S(2)}) copy-start(s32[1,48,8]{1,2,0:T(8,128)} %param.12) | copy-start | bytes 4612
  100.1 28.7 %copy-start.5 = (f32[1,48,128]{2,1,0:T(8,128)S(1)}, f32[1,48,128]{2,1,0:T(8,128)}, u32[]{:S(2)}) copy-start(f32[1,48,128]{2,1,0:T(8,128)} %param.11) | copy-start | bytes 73732
  100.2 29.9 %copy-start.7 = (bf16[24,2,256]{2,1,0:T(2,128)(2,1)S(1)}, bf16[24,2,256]{2,1,0:T(2,128)(2,1)}, u32[]{:S(2)}) copy-start(bf16[24,2,256]{2,1,0:T(2,128)(2,1)} %get-tuple-element.5) | copy-start | bytes 73732
  127.2 18.0 %copy-start.4 = (bf16[32,32,128]{2,1,0:T(8,128)(2,1)S(1)}, bf16[32,32,128]{2,1,0:T(8,128)(2,1)}, u32[]{:S(2)}) copy-start(bf16[32,32,128]{2,1,0:T(8,128)(2,1)} %shard_map.115) | copy-start | bytes 786436
  128.8 17.3 %copy-start.6 = (bf16[128,160]{0,1:T(8,128)(2,1)S(1)}, bf16[128,160]{0,1:T(8,128)(2,1)}, u32[]{:S(2)}) copy-start(bf16[128,160]{0,1:T(8,128)(2,1)} %param.14) | copy-start | bytes 122884

commit v2 on v0

v2 whole, which is shorter than its diff:
```python
import functools

import jax
import jax.numpy as jnp
from jax import lax
from jax.experimental import pallas as pl
from jax.experimental.pallas import tpu as pltpu
from jax.sharding import Mesh
from jax.sharding import PartitionSpec as P

DP = ("dp_0", "dp_1")
MESH = pl.DeviceIdType.MESH
VMEM = pl.BlockSpec(memory_space=pltpu.VMEM)
HBM = pl.BlockSpec(memory_space=pl.ANY)
F32, BF16 = jnp.float32, jnp.bfloat16
LANES = 128
TAIL = 32
PIECE = 32
CHUNK = 8

route_scale = 2.5


def iota(shape, dim):
    return lax.broadcasted_iota(jnp.int32, shape, dim)


def over(values, by):
    if by & (by - 1) == 0:
        return lax.shift_right_logical(values, jnp.full_like(values, by.bit_length() - 1))
    return lax.shift_right_logical(values * (65536 // by + 1), jnp.full_like(values, 16))


def hot_of(condition):
    return jnp.where(condition, 1.0, 0.0).astype(BF16)


def mm(a, b):
    return jnp.dot(a, b, preferred_element_type=F32)


def mm_nt(a, b):
    return lax.dot_general(a, b, (((1,), (1,)), ((), ())), preferred_element_type=F32)


def split_pair(values):
    upper = values.astype(BF16)
    return upper, (values - upper.astype(F32)).astype(BF16)


def layer_kernel(
    shape,
    rows_ref,
    ids_ref,
    logits_ref,
    router_ref,
    router_weight_ref,
    gate_hbm,
    up_hbm,
    down_hbm,
    saved_gate_hbm,
    saved_up_hbm,
    grad_input_ref,
    grad_router_ref,
    gate_w,
    up_w,
    down_w,
    saved_gate,
    saved_up,
    gate_factor,
    up_factor,
    hidden_ref,
    own_ref,
    sum_ref,
    send_buf,
    recv_buf,
    swap_buf,
    out_piece,
    in_piece,
    x_main,
    x_tail,
    part_gate,
    part_up,
    e_main,
    e_tail,
    g_upper,
    g_lower,
    back_out,
    back_in,
    mix_ref,
    got_ref,
    term_out,
    term_in,
    load_sem,
    send_sem,
    recv_sem,
    swap_send,
    swap_recv,
    gsend,
    grecv,
    piece_send,
    piece_recv,
    back_send,
    back_recv,
    term_send,
    term_recv,
    row_send,
    row_recv,
):
    count, ring, dp_1, local_experts, depth, parts = shape
    me, z, h = lax.axis_index("expert"), lax.axis_index("dp_0"), lax.axis_index("dp_1")
    dp_count = ring * dp_1
    mine = z * dp_1 + h
    tokens, experts = logits_ref.shape
    feature_share = LANES + TAIL
    half = ring // 2
    block_rows, width = own_ref.shape[1:]
    expert_rows = count * depth
    rows = block_rows // parts
    per_expert = expert_rows // block_rows
    per_device = tokens // dp_count
    gate_row = local_experts * depth + depth
    neighbour = ({"dp_0": lax.rem(z + 1, ring)}, {"dp_0": lax.rem(z + ring - 1, ring)})
    partner = {"dp_1": 1 - h}

    def loads():
        copies = []
        for n, (hbm, to) in enumerate(((down_hbm, down_w), (gate_hbm, gate_w), (up_hbm, up_w))):
            for e in range(local_experts):
                for part, (at, size, put) in enumerate(
                    ((0, LANES, 0), (LANES, TAIL, LANES + e * TAIL))
                ):
                    copies.append(
                        pltpu.make_async_copy(
                            hbm.at[e, pl.ds(at, size)],
                            to.at[e, pl.ds(put, size)],
                            load_sem.at[n * 2 * local_experts + 2 * e + part],
                        )
                    )
        last = 3 * 2 * local_experts
        copies.append(pltpu.make_async_copy(saved_gate_hbm, saved_gate, load_sem.at[last]))
        copies.append(pltpu.make_async_copy(saved_up_hbm, saved_up, load_sem.at[last + 1]))
        return copies

    load = loads()
    down_loads, late_loads, saved_loads = load[:8], load[8:24], load[24:]
    for copy in down_loads + saved_loads + late_loads:
        copy.start()

    barrier = pltpu.get_barrier_semaphore()

    def dp_peer(k):
        peer = lax.rem(mine + k, dp_count)
        return {"dp_0": peer // dp_1, "dp_1": lax.rem(peer, dp_1)}

    def greet_expert(k, carry):
        pl.semaphore_signal(
            barrier, inc=1, device_id={"expert": lax.rem(me + k, count)}, device_id_type=MESH
        )
        return carry

    def greet_dp(k, carry):
        pl.semaphore_signal(barrier, inc=1, device_id=dp_peer(k), device_id_type=MESH)
        return carry

    lax.fori_loop(1, dp_count, greet_dp, 0)
    lax.fori_loop(1, count, greet_expert, 0)

    for to in (down_w, gate_w, up_w):
        for e in range(local_experts):
            first = LANES + e * TAIL
            if e:
                to[e, LANES:first, :] = jnp.zeros((e * TAIL, width), BF16)
            if e < local_experts - 1:
                size = (local_experts - 1 - e) * TAIL
                to[e, first + TAIL : first + TAIL + size, :] = jnp.zeros((size, width), BF16)

    hot_t = jnp.zeros((experts, tokens), F32)
    for k in range(ids_ref.shape[0]):
        hot_t = hot_t + jnp.where(
            iota((experts, tokens), 0) == ids_ref[k : k + 1, :], 1.0, 0.0
        )
    earlier = hot_of(iota((tokens, tokens), 0) < iota((tokens, tokens), 1))
    ranked_t = (hot_t * (mm(hot_t.astype(BF16), earlier) + 1.0)).astype(BF16)

    main_rows = count * local_experts * depth
    row, col = iota((main_rows, experts), 0), iota((main_rows, experts), 1)
    values = mm(hot_of(over(row, depth) == col), ranked_t)
    wanted = iota((main_rows, tokens), 0)
    wanted = (wanted - over(wanted, depth) * depth + 1).astype(F32)
    piece_main = mm(hot_of(values == wanted), rows_ref[:, :LANES])
    tail_rows = count * 8
    row, col = iota((tail_rows, experts), 0), iota((tail_rows, experts), 1)
    rank_of = iota((tail_rows, tokens), 0)
    rank_of = rank_of - over(rank_of, 8) * 8
    wanted = jnp.where(rank_of < depth, rank_of + 1, depth + 1000).astype(F32)
    piece_tail = jnp.zeros((tail_rows, LANES), F32)
    for e in range(local_experts):
        values = mm(hot_of(over(row, 8) * local_experts + e == col), ranked_t)
        lanes = hot_of(iota((TAIL, LANES), 0) + e * TAIL == iota((TAIL, LANES), 1))
        placed = mm(rows_ref[:, LANES:feature_share], lanes).astype(BF16)
        piece_tail = piece_tail + mm(hot_of(values == wanted), placed)
    out_piece[...] = jnp.concatenate(
        [
            piece_main.reshape(count, local_experts * depth, LANES),
            piece_tail.reshape(count, 8, LANES),
        ],
        axis=1,
    ).astype(BF16)

    pl.semaphore_wait(barrier, count - 1 + dp_count - 1)

    def exchange(k, src, dst, send, recv):
        peer = lax.rem(me + k, count)
        return pltpu.make_async_remote_copy(
            src_ref=src.at[peer],
            dst_ref=dst.at[me],
            send_sem=send.at[k],
            recv_sem=recv.at[k],
            device_id={"expert": peer},
            device_id_type=MESH,
        )

    def start_exchange(*refs):
        def start(k, carry):
            exchange(k, *refs).start()
            return carry

        lax.fori_loop(1, count, start, 0)

    def wait_exchange(*refs):
        def wait(k, carry):
            exchange(k, *refs).wait()
            return carry

        lax.fori_loop(1, count, wait, 0)

    piece = (out_piece, in_piece, piece_send, piece_recv)
    back = (back_out, back_in, back_send, back_recv)
    term = (term_out, term_in, term_send, term_recv)
    start_exchange(*piece)
    in_piece[me] = out_piece[me]

    def window(peer):
        return pl.multiple_of(peer * feature_share // LANES * LANES, LANES)

    def row_copy(k):
        peer = lax.rem(mine + k, dp_count)
        return pltpu.make_async_remote_copy(
            src_ref=router_ref.at[:, pl.ds(window(peer), 2 * LANES)],
            dst_ref=got_ref.at[mine],
            send_sem=row_send.at[k],
            recv_sem=row_recv.at[k],
            device_id=dp_peer(k),
            device_id_type=MESH,
        )

    def start_row(k, carry):
        row_copy(k).start()
        return carry

    def wait_row(k, carry):
        row_copy(k).wait()
        return carry

    lax.fori_loop(1, dp_count, start_row, 0)
    got_ref[mine] = router_ref[:, pl.ds(window(mine), 2 * LANES)]

    same = hot_of(iota((tokens, tokens), 0) == iota((tokens, tokens), 1))
    ranked = mm_nt(same, ranked_t)
    hot = jnp.where(ranked > 0.0, 1.0, 0.0)
    scores = 1.0 / (1.0 + jnp.exp(-logits_ref[...]))
    total = jnp.sum(scores * hot, axis=1, keepdims=True)
    gates = route_scale * (scores * hot) / total
    gate_upper, gate_lower = split_pair(gates)
    ranked_b = ranked.astype(BF16)
    span = count * PIECE
    slot = iota((experts, span), 1)
    inside = slot - over(slot, PIECE) * PIECE
    named = iota((experts, span), 0)
    line = iota((tokens, span), 1)
    line = line - over(line, PIECE) * PIECE
    line_rank = line - over(line, depth) * depth
    for e in range(local_experts + 1):
        if e == local_experts:
            of_expert = over(slot, PIECE) * local_experts + over(inside, depth)
            take = inside < local_experts * depth
            wanted = jnp.where(line < local_experts * depth, line_rank + 1, depth + 1000)
        else:
            of_expert = over(slot, PIECE) * local_experts + e
            take = (inside >= local_experts * depth) & (inside < gate_row)
            wanted = jnp.where(
                (line >= local_experts * depth) & (line < gate_row), line_rank + 1, depth + 1000
            )
        spread = hot_of((of_expert == named) & take)
        holds = mm(ranked_b, spread) == wanted.astype(F32)
        for n, part in enumerate((gate_upper, gate_lower)):
            at = (2 * e + n) * tokens
            mix_ref[at : at + tokens, :] = jnp.where(holds, mm(part, spread), 0.0).astype(BF16)

    for copy in saved_loads:
        copy.wait()

    def factors(block):
        def some(n, carry):
            at = pl.ds(pl.multiple_of(n * 16, 16), 16)
            gate_value = saved_gate[block, at, :].astype(F32)
            up_value = saved_up[block, at, :].astype(F32)
            sigmoid = 1.0 / (1.0 + jnp.exp(-gate_value))
            active = gate_value * sigmoid
            hidden_ref[block, at, :] = (active * up_value).astype(BF16)
            gate_factor[block, at, :] = (
                up_value * sigmoid * (1.0 + gate_value * (1.0 - sigmoid))
            )
            up_factor[block, at, :] = active
            return carry

        lax.fori_loop(0, block_rows // 16, some, 0)

    early = max(ring - half - 2, 0)
    for block in range(early):
        factors(block)

    chunk_rows = CHUNK * depth
    order_rows = (local_experts + 1) * chunk_rows

    def source(values):
        of_expert = over(values, chunk_rows)
        within = values - of_expert * chunk_rows
        group = over(within, depth)
        return group * PIECE + of_expert * depth + within - group * depth

    order_in = hot_of(
        source(iota((order_rows, CHUNK * PIECE), 0)) == iota((order_rows, CHUNK * PIECE), 1)
    )
    for copy in down_loads:
        copy.wait()
    wait_exchange(*piece)
    for n in range(count // CHUNK):
        chunk = in_piece[n * CHUNK : (n + 1) * CHUNK].reshape(CHUNK * PIECE, LANES)
        ordered = mm(order_in, chunk).astype(BF16)
        for e in range(local_experts):
            at = e * expert_rows + n * chunk_rows
            x_main[at : at + chunk_rows, :] = ordered[e * chunk_rows : (e + 1) * chunk_rows]
        x_tail[n * chunk_rows : (n + 1) * chunk_rows, :] = ordered[local_experts * chunk_rows :]

    def at(way, distance):
        step = distance if way == 0 else ring - distance
        return lax.rem(z + step, ring)

    def part(g):
        return pl.ds(g * rows, rows)

    def runs(way, distance, g):
        if distance < half:
            return True
        return (g < parts // 2) == (way == 0)

    def hop(way, step, g):
        return pltpu.make_async_remote_copy(
            src_ref=send_buf.at[way, step, part(g)],
            dst_ref=recv_buf.at[way, step, part(g)],
            send_sem=send_sem.at[way, step, g],
            recv_sem=recv_sem.at[way, step, g],
            device_id=neighbour[way],
            device_id_type=MESH,
        )

    def swap(g):
        return pltpu.make_async_remote_copy(
            src_ref=swap_buf.at[0, part(g)],
            dst_ref=swap_buf.at[1, part(g)],
            send_sem=swap_send.at[g],
            recv_sem=swap_recv.at[g],
            device_id=partner,
            device_id_type=MESH,
        )

    def gather(way, step, g):
        block = at(1 - way, step) if step else z
        return pltpu.make_async_remote_copy(
            src_ref=sum_ref.at[block, part(g)],
            dst_ref=sum_ref.at[block, part(g)],
            send_sem=gsend.at[way, step, g],
            recv_sem=grecv.at[way, step, g],
            device_id=neighbour[way],
            device_id_type=MESH,
        )

    far = lax.rem(z + half, ring)
    far_expert = far // per_expert
    far_tail = pl.ds(pl.multiple_of(lax.rem(far, per_expert) * block_rows, block_rows), block_rows)
    far_rows = pl.ds(pl.multiple_of(far * block_rows, block_rows), block_rows)
    first = jnp.concatenate([x_main[far_rows, :], x_tail[far_tail, :]], axis=1)
    first = mm(first, down_w[far_expert]).astype(BF16)
    for way in range(2):
        for g in range(parts):
            if runs(way, half, g):
                send_buf[way, 0, part(g), :] = first[g * rows : (g + 1) * rows]
                hop(way, 0, g).start()
    for e in range(local_experts):
        inputs = jnp.concatenate(
            [x_main[e * expert_rows : (e + 1) * expert_rows, :], x_tail[...]], axis=1
        )
        terms = mm(inputs, down_w[e])
        for n in range(per_expert):
            own_ref[e * per_expert + n] = terms[n * block_rows : (n + 1) * block_rows]

    for step in range(1, half):
        distance = half - step
        for g in range(parts):
            for way in range(2):
                value = own_ref[at(way, distance), part(g), :]
                if runs(way, distance + 1, g):
                    hop(way, step - 1, g).wait_recv()
                    value = value + recv_buf[way, step - 1, part(g), :].astype(F32)
                send_buf[way, step, part(g), :] = value.astype(BF16)
                hop(way, step, g).start()
        if early + step - 1 < ring:
            factors(early + step - 1)
    for g in range(parts):
        value = own_ref[z, part(g), :]
        for way in range(2):
            if runs(way, 1, g):
                hop(way, half - 1, g).wait_recv()
                value = value + recv_buf[way, half - 1, part(g), :].astype(F32)
        own_ref[z, part(g), :] = value
        swap_buf[0, part(g), :] = value.astype(BF16)
        swap(g).start()
    for block in range(early + half - 1, ring):
        factors(block)
    for copy in late_loads:
        copy.wait()
    e_tail[...] = jnp.zeros_like(e_tail)
    for g in range(parts):
        swap(g).wait_recv()
        total_sum = own_ref[z, part(g), :] + swap_buf[1, part(g), :].astype(F32)
        sum_ref[z, part(g), :] = total_sum.astype(BF16)
        for way in range(2):
            if runs(way, 1, g):
                gather(way, 0, g).start()

    def project(block):
        of_expert = block // per_expert
        first_row = lax.rem(block, per_expert) * block_rows
        gate_rows = []
        for n in range(block_rows // 16):
            cut = slice(n * 16, (n + 1) * 16)
            value = sum_ref[block, cut, :].astype(F32)
            gate_rows.append(
                jnp.sum(hidden_ref[block, cut, :].astype(F32) * value, axis=1, keepdims=True)
            )
            part_gate[cut, :] = (value * gate_factor[block, cut, :]).astype(BF16)
            part_up[cut, :] = (value * up_factor[block, cut, :]).astype(BF16)
        gate_sum = jnp.concatenate(gate_rows, axis=0)
        out = mm_nt(part_gate[...], gate_w[of_expert]) + mm_nt(part_up[...], up_w[of_expert])
        block_at = pl.ds(pl.multiple_of(block * block_rows, block_rows), block_rows)
        tail_at = pl.ds(pl.multiple_of(first_row, block_rows), block_rows)
        e_main[block_at, :] = out[:, :LANES].astype(BF16)
        e_tail[tail_at, :] = e_tail[tail_at, :] + out[:, LANES:]
        place = iota((block_rows, LANES), 0) + first_row
        place = place - over(place, depth) * depth + of_expert * depth
        held = place == iota((block_rows, LANES), 1)
        upper, lower = split_pair(jnp.broadcast_to(gate_sum, (block_rows, LANES)))
        zero = jnp.zeros((block_rows, LANES), F32)
        g_upper[block_at, :] = jnp.where(held, upper.astype(F32), zero).astype(BF16)
        g_lower[block_at, :] = jnp.where(held, lower.astype(F32), zero).astype(BF16)

    project(z)
    for step in range(1, half):
        for g in range(parts):
            for way in range(2):
                gather(way, step - 1, g).wait_recv()
                if runs(way, step + 1, g):
                    gather(way, step, g).start()

        def arrived(way, carry):
            project(lax.rem(z + jnp.where(way == 0, ring - step, step), ring))
            return carry

        lax.fori_loop(0, 2, arrived, 0)
    for g in range(parts):
        for way in range(2):
            if runs(way, half, g):
                gather(way, half - 1, g).wait_recv()
    project(far)

    piece_of = iota((CHUNK * PIECE, order_rows), 0)
    order_out = hot_of(source(iota((CHUNK * PIECE, order_rows), 1)) == piece_of)
    gate_cols = local_experts * chunk_rows
    group_of = iota((CHUNK * PIECE, gate_cols), 1)
    group_of = over(group_of - over(group_of, chunk_rows) * chunk_rows, depth) * PIECE
    piece_of = iota((CHUNK * PIECE, gate_cols), 0)
    order_upper = hot_of(group_of + gate_row == piece_of)
    order_lower = hot_of(group_of + gate_row + 1 == piece_of)
    for n in range(count // CHUNK):

        def cut(ref):
            return [
                ref[e * expert_rows + n * chunk_rows : e * expert_rows + (n + 1) * chunk_rows, :]
                for e in range(local_experts)
            ]

        tail = e_tail[n * chunk_rows : (n + 1) * chunk_rows, :].astype(BF16)
        pieces = mm(order_out, jnp.concatenate([*cut(e_main), tail], axis=0))
        pieces = pieces + mm(order_upper, jnp.concatenate(cut(g_upper), axis=0))
        pieces = pieces + mm(order_lower, jnp.concatenate(cut(g_lower), axis=0))
        back_out[n * CHUNK : (n + 1) * CHUNK] = pieces.astype(BF16).reshape(CHUNK, PIECE, LANES)
    start_exchange(*back)
    back_in[me] = back_out[me]

    gate_lines = iota((count, span), 1) - iota((count, span), 0) * PIECE
    pick_lines = hot_of((gate_lines == gate_row) | (gate_lines == gate_row + 1))
    lane, to = iota((LANES, depth * experts), 0), iota((LANES, depth * experts), 1)
    to_rank = over(to, experts)
    to_expert = to - to_rank * experts
    to_local = to_expert - over(to_expert, local_experts) * local_experts
    to_lane = hot_of(lane == to_local * depth + to_rank)
    to = iota((count, depth * experts), 1)
    to_expert = to - over(to, experts) * experts
    from_owner = over(to_expert, local_experts) == iota((count, depth * experts), 0)
    line8 = iota((count * 8, experts), 0)
    owner8 = over(line8, 8)
    inner8 = line8 - owner8 * 8
    inner8 = inner8 - over(inner8, local_experts) * local_experts
    repeat8 = hot_of(owner8 * local_experts + inner8 == iota((count * 8, experts), 1))
    token8 = iota((tokens, dp_count * 8), 1)
    inner = token8 - over(token8, 8) * 8
    widen = hot_of(
        (over(token8, 8) * per_device + inner == iota((tokens, dp_count * 8), 0))
        & (inner < per_device)
    )
    lax.fori_loop(1, dp_count, wait_row, 0)
    grouped = got_ref[...].astype(F32).reshape(dp_count * 8, 2 * LANES).astype(BF16)

    wait_exchange(*back)
    landed = back_in[...].reshape(span, LANES)
    lines_upper, lines_lower = split_pair(mm(pick_lines, landed))
    by_rank = mm(lines_upper, to_lane) + mm(lines_lower, to_lane)
    by_rank = jnp.sum(jnp.where(from_owner, by_rank, 0.0), axis=0, keepdims=True)
    picked = jnp.zeros((tokens, experts), F32)
    for r in range(depth):
        picked = picked + jnp.where(
            ranked == float(r + 1), by_rank[:, r * experts : (r + 1) * experts], 0.0
        )
    mixture = jnp.sum(picked * gates, axis=1, keepdims=True)
    d_chosen = hot * (route_scale * picked - mixture) / total
    logit_grad = (d_chosen * scores * (1.0 - scores)).astype(BF16)
    spread8 = mm(mm_nt(repeat8, logit_grad).astype(BF16), widen).astype(BF16)
    terms = mm(spread8, grouped)
    shift = lax.rem(mine * feature_share, LANES)
    terms = pltpu.roll(terms, lax.rem(2 * LANES - shift, 2 * LANES), 1)
    line8 = iota((count * 8, LANES), 0)
    line8 = line8 - over(line8, 8) * 8
    term_out[...] = jnp.where(
        line8 < local_experts, terms[:, :LANES], terms[:, LANES:]
    ).reshape(count, 8, LANES)
    start_exchange(*term)
    term_in[me] = term_out[me]

    mixed = mm(mix_ref[...], landed)
    lane_of = over(iota((tokens, LANES), 1), TAIL)
    tails = jnp.zeros((tokens, LANES), F32)
    for e in range(local_experts):
        at_row = 2 * e * tokens
        both = mixed[at_row : at_row + tokens] + mixed[at_row + tokens : at_row + 2 * tokens]
        tails = tails + jnp.where(lane_of == e, both, 0.0)
    folded = tails
    for e in range(1, local_experts):
        folded = folded + pltpu.roll(tails, LANES - e * TAIL, 1)
    at_row = 2 * local_experts * tokens
    main = mixed[at_row : at_row + tokens] + mixed[at_row + tokens : at_row + 2 * tokens]
    main = main + mm_nt(logit_grad, router_weight_ref[:LANES, :])
    side = folded[:, :TAIL] + mm_nt(logit_grad, router_weight_ref[LANES:feature_share, :])
    grad_input_ref[:, :LANES] = main.astype(BF16)
    grad_input_ref[:, LANES:feature_share] = side.astype(BF16)

    for step in range(half):
        for g in range(parts):
            for way in range(2):
                if runs(way, half - step, g):
                    hop(way, step, g).wait_send()
                if runs(way, step + 1, g):
                    gather(way, step, g).wait_send()
    for g in range(parts):
        swap(g).wait_send()

    wait_exchange(*term)
    sums = jnp.sum(term_in[...], axis=0)
    grad_router_ref[:, :LANES] = sums[:local_experts]
    grad_router_ref[:, LANES:feature_share] = sums[local_experts : 2 * local_experts, :TAIL]


def local(
    grad_output,
    router_logits,
    expert_ids,
    router_input,
    router_weight,
    gate_weight,
    up_weight,
    down_weight,
    gate_saved,
    up_saved,
):
    count = lax.axis_size("expert")
    ring, dp_1 = lax.axis_size("dp_0"), lax.axis_size("dp_1")
    dp_count = ring * dp_1
    tokens, feature_share = grad_output.shape[1:]
    experts = router_logits.shape[2]
    local_experts, slot_count, width = gate_saved.shape
    depth = slot_count // count
    expert_rows = slot_count
    row_total = local_experts * slot_count
    block_rows = row_total // ring
    parts = block_rows // 16
    half = ring // 2
    span = count * PIECE
    blocked = (ring, block_rows, width)
    hops = pltpu.SemaphoreType.DMA((2, half, parts))
    swaps = pltpu.SemaphoreType.DMA((parts,))
    peers = pltpu.SemaphoreType.DMA((count,))
    dp_peers = pltpu.SemaphoreType.DMA((dp_count,))
    router_rows = jnp.pad(router_input[0], ((0, 8 - tokens // dp_count), (0, 0)))
    grad_input, grad_router = pl.pallas_call(
        functools.partial(layer_kernel, (count, ring, dp_1, local_experts, depth, parts)),
        out_shape=(
            jax.ShapeDtypeStruct((tokens, feature_share), BF16),
            jax.ShapeDtypeStruct((local_experts, feature_share), F32),
        ),
        in_specs=[VMEM] * 5 + [HBM] * 5,
        out_specs=(VMEM, VMEM),
        scratch_shapes=[
            pltpu.VMEM((local_experts, 2 * LANES, width), BF16),
            pltpu.VMEM((local_experts, 2 * LANES, width), BF16),
            pltpu.VMEM((local_experts, 2 * LANES, width), BF16),
            pltpu.VMEM(blocked, BF16),
            pltpu.VMEM(blocked, BF16),
            pltpu.VMEM(blocked, F32),
            pltpu.VMEM(blocked, F32),
            pltpu.VMEM(blocked, BF16),
            pltpu.VMEM(blocked, F32),
            pltpu.VMEM(blocked, BF16),
            pltpu.VMEM((2, half, block_rows, width), BF16),
            pltpu.VMEM((2, half, block_rows, width), BF16),
            pltpu.VMEM((2, block_rows, width), BF16),
            pltpu.VMEM((count, PIECE, LANES), BF16),
            pltpu.VMEM((count, PIECE, LANES), BF16),
            pltpu.VMEM((row_total, LANES), BF16),
            pltpu.VMEM((expert_rows, LANES), BF16),
            pltpu.VMEM((block_rows, width), BF16),
            pltpu.VMEM((block_rows, width), BF16),
            pltpu.VMEM((row_total, LANES), BF16),
            pltpu.VMEM((expert_rows, LANES), F32),
            pltpu.VMEM((row_total, LANES), BF16),
            pltpu.VMEM((row_total, LANES), BF16),
            pltpu.VMEM((count, PIECE, LANES), BF16),
            pltpu.VMEM((count, PIECE, LANES), BF16),
            pltpu.VMEM(((local_experts + 1) * 2 * tokens, span), BF16),
            pltpu.VMEM((dp_count, 8, 2 * LANES), BF16),
            pltpu.VMEM((count, 8, LANES), F32),
            pltpu.VMEM((count, 8, LANES), F32),
            pltpu.SemaphoreType.DMA((3 * 2 * local_experts + 2,)),
            hops,
            hops,
            swaps,
            swaps,
            hops,
            hops,
            peers,
            peers,
            peers,
            peers,
            peers,
            peers,
            dp_peers,
            dp_peers,
        ],
        compiler_params=pltpu.CompilerParams(
            collective_id=0, has_side_effects=True, vmem_limit_bytes=60 << 20
        ),
    )(
        grad_output[0],
        expert_ids[0].T,
        router_logits[0],
        router_rows,
        router_weight.T,
        gate_weight,
        up_weight,
        jnp.swapaxes(down_weight, 1, 2),
        gate_saved.reshape(blocked),
        up_saved.reshape(blocked),
    )
    return (grad_input[None], grad_router)


def solution(mesh):
    torus = Mesh(
        mesh.devices.reshape(mesh.shape["dp"] // 2, 2, mesh.shape["expert"]),
        ("dp_0", "dp_1", "expert"),
    )
    placed = (
        P("expert", None, DP),
        P("expert", None, None),
        P("expert", None, None),
        P("expert", DP, None),
        P(None, DP),
        P("expert", DP, None),
        P("expert", DP, None),
        P("expert", None, DP),
        P("expert", None, None),
        P("expert", None, None),
    )
    return jax.shard_map(
        local,
        mesh=torus,
        in_specs=placed,
        out_specs=(P("expert", None, DP), P("expert", DP)),
        check_vma=False,
    )
```

time: 319 us -> 103 us (0.32)
  waiting for transfers between devices: 226 us -> 0 us
  Pallas kernels: 0 us -> 98.4 us
  starting transfers between devices: 29.8 us -> 0 us
  blocking collectives: 24.3 us -> 0 us
  between operations: 14.1 us -> 0.64 us
  local copies, waits for them, and re-layouts: 11.2 us -> 3.97 us
  matrix products: 7.01 us -> 0 us
  other arithmetic: 5.91 us -> 0 us
    all_gather x1 -> x0, waiting for transfers between devices: 116 us -> none  [in_one_piece(): whole = lax.all_gather(both, axis, axis=dim, tiled=True)]
    pallas_call x0 -> x1, Pallas kernels: none -> 98.4 us  [local(): pl.pallas_call(functools.partial(layer_kernel, (count, ring, dp_1, local_...]
    unnamed x4 -> x0, waiting for transfers between devices: 56.9 us -> none
    reduce_scatter x1 -> x0, waiting for transfers between devices: 32.1 us -> none  [sum_by_axis(): shard = lax.psum_scatter(shard, axis, scatter_dimension=dim, tiled=True)]
    all_to_all x3 -> x0, starting transfers between devices: 29.7 us -> none  [the longest x1 14.3 us: in_one_piece_2(): lax.all_to_all(both, axis, split_axis=split_dim, concat_axis=concat_dim,...]
    all_to_all x1 -> x0, blocking collectives: 24.3 us -> none  [local(): lax.all_to_all(outgoing.reshape(expert_total, slot_depth, feature_share),...]
    all_to_all x3 -> x0, waiting for transfers between devices: 21.1 us -> none  [the longest x1 12.9 us: in_one_piece_2(): lax.all_to_all(both, axis, split_axis=split_dim, concat_axis=concat_dim,...]
    dot_general x8 -> x0, matrix products: 7.01 us -> none  [the longest x1 2.24 us: local(): jnp.einsum('esd,efd->esf', incoming, down_weight, preferred_element_type=...]
  transfers between devices with their start and end apart: 6 -> 0, of which waited for: 5 -> 0; matrix products, arithmetic and copies ran while one was open for 3% -> 0% of each run, Pallas kernels for 0% -> 0%
where the time goes in v2:
time: 103 us
  Pallas kernels  98.4 us (96%)
  local copies, waits for them, and re-layouts  3.97 us (4%)
    pallas_call x1, Pallas kernels, local(): pl.pallas_call(functools.partial(layer_kernel, (count, ring, dp_1, local_...  98.4 us
    unnamed x2, local copies, waits for them, and re-layouts  2.62 us

profile of v2, /device:TPU:1, one launch (start us, length us, event | category | flops | bytes accessed | tf_op | source)
XLA Modules:
  0.0 103.0 jit_solution(17491681944654447794)
XLA Ops:
  0.6 1.3 %pad.4.router_ref = bf16[8,3840]{1,0:T(8,128)(2,1)} pad(bf16[2,3840]{1,0:T(2,128)(2,1)} %bitcast.18, bf16[]{:T(256)} %constant.2.clone.1), padding=0_6x0_0 | pad | bytes 76802 | tf_op jit(solution)/shard_map/jit(_pad)/pad | solution.py:624
  2.0 98.4 %shard_map.113 = (bf16[48,160]{1,0:T(8,128)(2,1)}, f32[4,160]{1,0:T(4,128)}) custom-call(bf16[48,160]{1,0:T(8,128)(2,1)} %bitcast.16, s32[8,48]{1,0:T(8,128)} %bitcast.19, f32[48,128]{1,0:T(8,128)} %bitcast.17, bf16[8,3840]{1,0:T(8,128)(2,1)} %pad.4.router_ref, bf16[160,128]{1,0:T(8,128)(2,1)} %bitcast.14, bf16[4,160,1024]{2,1,0:T(8,128)(2,1)} %gate_hbm.1, ...), custom_call_target="tpu_custom_call" | custom-call | tf_op jit(solution)/shard_map/pallas_call | solution.py:625
  100.3 1.3 %copy.14 = bf16[1,48,160]{2,1,0:T(8,128)(2,1)} copy(bf16[1,48,160]{2,1,0:T(8,128)(2,1)} %bitcast.15) | data formatting | bytes 30720
  101.7 1.3 %copy.15 = f32[4,160]{1,0:T(4,128)} copy(f32[4,160]{1,0:T(4,128)} %get-tuple-element.9) | data formatting | bytes 5120

commit v3 on v2

--- a/solution.py
+++ b/solution.py
@@ -50,11 +50,11 @@
 
 def layer_kernel(
     shape,
-    rows_ref,
-    ids_ref,
-    logits_ref,
-    router_ref,
-    router_weight_ref,
+    rows_hbm,
+    ids_hbm,
+    logits_hbm,
+    router_hbm,
+    router_weight_hbm,
     gate_hbm,
     up_hbm,
     down_hbm,
@@ -62,6 +62,12 @@
     saved_up_hbm,
     grad_input_ref,
     grad_router_ref,
+    rows_ref,
+    ids_ref,
+    logits_ref,
+    router_in,
+    router_weight_ref,
+    router_ref,
     gate_w,
     up_w,
     down_w,
@@ -85,12 +91,15 @@
     e_tail,
     g_upper,
     g_lower,
+    gate_out,
+    gate_in,
     back_out,
     back_in,
     mix_ref,
     got_ref,
     term_out,
     term_in,
+    small_sem,
     load_sem,
     send_sem,
     recv_sem,
@@ -100,6 +109,8 @@
     grecv,
     piece_send,
     piece_recv,
+    gate_send,
+    gate_recv,
     back_send,
     back_recv,
     term_send,
@@ -111,7 +122,7 @@
     me, z, h = lax.axis_index("expert"), lax.axis_index("dp_0"), lax.axis_index("dp_1")
     dp_count = ring * dp_1
     mine = z * dp_1 + h
-    tokens, experts = logits_ref.shape
+    tokens, experts = logits_hbm.shape
     feature_share = LANES + TAIL
     half = ring // 2
     block_rows, width = own_ref.shape[1:]
@@ -142,39 +153,45 @@
         copies.append(pltpu.make_async_copy(saved_up_hbm, saved_up, load_sem.at[last + 1]))
         return copies
 
+    small = [
+        pltpu.make_async_copy(hbm, to, small_sem.at[n])
+        for n, (hbm, to) in enumerate(
+            (
+                (ids_hbm, ids_ref),
+                (rows_hbm, rows_ref),
+                (router_hbm, router_in),
+                (logits_hbm, logits_ref),
+                (router_weight_hbm, router_weight_ref),
+            )
+        )
+    ]
+    for copy in small:
+        copy.start()
+
+    barrier = pltpu.get_barrier_semaphore()
+
+    def dp_peer(k):
+        peer = lax.rem(mine + k, dp_count)
+        return {"dp_0": peer // dp_1, "dp_1": lax.rem(peer, dp_1)}
+
+    def greet_expert(k, carry):
+        pl.semaphore_signal(
+            barrier, inc=1, device_id={"expert": lax.rem(me + k, count)}, device_id_type=MESH
+        )
+        return carry
+
+    def greet_dp(k, carry):
+        pl.semaphore_signal(barrier, inc=1, device_id=dp_peer(k), device_id_type=MESH)
+        return carry
+
+    lax.fori_loop(1, dp_count, greet_dp, 0)
+    lax.fori_loop(1, count, greet_expert, 0)
     load = loads()
     down_loads, late_loads, saved_loads = load[:8], load[8:24], load[24:]
     for copy in down_loads + saved_loads + late_loads:
         copy.start()
 
-    barrier = pltpu.get_barrier_semaphore()
-
-    def dp_peer(k):
-        peer = lax.rem(mine + k, dp_count)
-        return {"dp_0": peer // dp_1, "dp_1": lax.rem(peer, dp_1)}
-
-    def greet_expert(k, carry):
-        pl.semaphore_signal(
-            barrier, inc=1, device_id={"expert": lax.rem(me + k, count)}, device_id_type=MESH
-        )
-        return carry
-
-    def greet_dp(k, carry):
-        pl.semaphore_signal(barrier, inc=1, device_id=dp_peer(k), device_id_type=MESH)
-        return carry
-
-    lax.fori_loop(1, dp_count, greet_dp, 0)
-    lax.fori_loop(1, count, greet_expert, 0)
-
-    for to in (down_w, gate_w, up_w):
-        for e in range(local_experts):
-            first = LANES + e * TAIL
-            if e:
-                to[e, LANES:first, :] = jnp.zeros((e * TAIL, width), BF16)
-            if e < local_experts - 1:
-                size = (local_experts - 1 - e) * TAIL
-                to[e, first + TAIL : first + TAIL + size, :] = jnp.zeros((size, width), BF16)
-
+    small[0].wait()
     hot_t = jnp.zeros((experts, tokens), F32)
     for k in range(ids_ref.shape[0]):
         hot_t = hot_t + jnp.where(
@@ -188,6 +205,7 @@
     values = mm(hot_of(over(row, depth) == col), ranked_t)
     wanted = iota((main_rows, tokens), 0)
     wanted = (wanted - over(wanted, depth) * depth + 1).astype(F32)
+    small[1].wait()
     piece_main = mm(hot_of(values == wanted), rows_ref[:, :LANES])
     tail_rows = count * 8
     row, col = iota((tail_rows, experts), 0), iota((tail_rows, experts), 1)
@@ -208,6 +226,15 @@
         axis=1,
     ).astype(BF16)
 
+    small[2].wait()
+    router_ref[...] = jnp.concatenate(
+        [
+            router_in[...].astype(F32),
+            jnp.zeros((8 - per_device, router_in.shape[1]), F32),
+        ],
+        axis=0,
+    ).astype(BF16)
+
     pl.semaphore_wait(barrier, count - 1 + dp_count - 1)
 
     def exchange(k, src, dst, send, recv):
@@ -236,6 +263,7 @@
         lax.fori_loop(1, count, wait, 0)
 
     piece = (out_piece, in_piece, piece_send, piece_recv)
+    early_gate = (gate_out, gate_in, gate_send, gate_recv)
     back = (back_out, back_in, back_send, back_recv)
     term = (term_out, term_in, term_send, term_recv)
     start_exchange(*piece)
@@ -265,6 +293,17 @@
 
     lax.fori_loop(1, dp_count, start_row, 0)
     got_ref[mine] = router_ref[:, pl.ds(window(mine), 2 * LANES)]
+
+    for copy in small[3:]:
+        copy.wait()
+    for to in (down_w, gate_w, up_w):
+        for e in range(local_experts):
+            first = LANES + e * TAIL
+            if e:
+                to[e, LANES:first, :] = jnp.zeros((e * TAIL, width), BF16)
+            if e < local_experts - 1:
+                size = (local_experts - 1 - e) * TAIL
+                to[e, first + TAIL : first + TAIL + size, :] = jnp.zeros((size, width), BF16)
 
     same = hot_of(iota((tokens, tokens), 0) == iota((tokens, tokens), 1))
     ranked = mm_nt(same, ranked_t)
@@ -440,7 +479,7 @@
             if runs(way, 1, g):
                 gather(way, 0, g).start()
 
-    def project(block):
+    def activate(block):
         of_expert = block // per_expert
         first_row = lax.rem(block, per_expert) * block_rows
         gate_rows = []
@@ -453,11 +492,7 @@
             part_gate[cut, :] = (value * gate_factor[block, cut, :]).astype(BF16)
             part_up[cut, :] = (value * up_factor[block, cut, :]).astype(BF16)
         gate_sum = jnp.concatenate(gate_rows, axis=0)
-        out = mm_nt(part_gate[...], gate_w[of_expert]) + mm_nt(part_up[...], up_w[of_expert])
         block_at = pl.ds(pl.multiple_of(block * block_rows, block_rows), block_rows)
-        tail_at = pl.ds(pl.multiple_of(first_row, block_rows), block_rows)
-        e_main[block_at, :] = out[:, :LANES].astype(BF16)
-        e_tail[tail_at, :] = e_tail[tail_at, :] + out[:, LANES:]
         place = iota((block_rows, LANES), 0) + first_row
         place = place - over(place, depth) * depth + of_expert * depth
         held = place == iota((block_rows, LANES), 1)
@@ -466,51 +501,69 @@
         g_upper[block_at, :] = jnp.where(held, upper.astype(F32), zero).astype(BF16)
         g_lower[block_at, :] = jnp.where(held, lower.astype(F32), zero).astype(BF16)
 
-    project(z)
+    def multiply(block):
+        of_expert = block // per_expert
+        first_row = lax.rem(block, per_expert) * block_rows
+        out = mm_nt(part_gate[...], gate_w[of_expert]) + mm_nt(part_up[...], up_w[of_expert])
+        block_at = pl.ds(pl.multiple_of(block * block_rows, block_rows), block_rows)
+        tail_at = pl.ds(pl.multiple_of(first_row, block_rows), block_rows)
+        e_main[block_at, :] = out[:, :LANES].astype(BF16)
+        e_tail[tail_at, :] = e_tail[tail_at, :] + out[:, LANES:]
+
+    def project(block):
+        activate(block)
+        multiply(block)
+
+    waiting = [z]
     for step in range(1, half):
         for g in range(parts):
             for way in range(2):
                 gather(way, step - 1, g).wait_recv()
                 if runs(way, step + 1, g):
                     gather(way, step, g).start()
-
-        def arrived(way, carry):
-            project(lax.rem(z + jnp.where(way == 0, ring - step, step), ring))
-            return carry
-
-        lax.fori_loop(0, 2, arrived, 0)
+            if g in (parts // 2 - 1, parts - 1) and waiting:
+                project(waiting.pop(0))
+        waiting += [at(1, step), at(0, step)]
+    for block in waiting:
+        project(block)
+
+    chunk_lines = CHUNK * 8
+    gate_cols = local_experts * chunk_rows
+    group_of = iota((chunk_lines, gate_cols), 1)
+    group_of = over(group_of - over(group_of, chunk_rows) * chunk_rows, depth) * 8
+    line_of = iota((chunk_lines, gate_cols), 0)
+    order_upper = hot_of(group_of == line_of)
+    order_lower = hot_of(group_of + 1 == line_of)
+    piece_of = iota((CHUNK * PIECE, order_rows), 0)
+    order_out = hot_of(source(iota((CHUNK * PIECE, order_rows), 1)) == piece_of)
+
+    def cut_of(ref, n):
+        return [
+            ref[e * expert_rows + n * chunk_rows : e * expert_rows + (n + 1) * chunk_rows, :]
+            for e in range(local_experts)
+        ]
+
     for g in range(parts):
         for way in range(2):
             if runs(way, half, g):
                 gather(way, half - 1, g).wait_recv()
-    project(far)
-
-    piece_of = iota((CHUNK * PIECE, order_rows), 0)
-    order_out = hot_of(source(iota((CHUNK * PIECE, order_rows), 1)) == piece_of)
-    gate_cols = local_experts * chunk_rows
-    group_of = iota((CHUNK * PIECE, gate_cols), 1)
-    group_of = over(group_of - over(group_of, chunk_rows) * chunk_rows, depth) * PIECE
-    piece_of = iota((CHUNK * PIECE, gate_cols), 0)
-    order_upper = hot_of(group_of + gate_row == piece_of)
-    order_lower = hot_of(group_of + gate_row + 1 == piece_of)
+    activate(far)
     for n in range(count // CHUNK):
-
-        def cut(ref):
-            return [
-                ref[e * expert_rows + n * chunk_rows : e * expert_rows + (n + 1) * chunk_rows, :]
-                for e in range(local_experts)
-            ]
-
+        lines = mm(order_upper, jnp.concatenate(cut_of(g_upper, n), axis=0))
+        lines = lines + mm(order_lower, jnp.concatenate(cut_of(g_lower, n), axis=0))
+        gate_out[n * CHUNK : (n + 1) * CHUNK] = lines.reshape(CHUNK, 8, LANES).astype(BF16)
+    start_exchange(*early_gate)
+    gate_in[me] = gate_out[me]
+    multiply(far)
+    for n in range(count // CHUNK):
         tail = e_tail[n * chunk_rows : (n + 1) * chunk_rows, :].astype(BF16)
-        pieces = mm(order_out, jnp.concatenate([*cut(e_main), tail], axis=0))
-        pieces = pieces + mm(order_upper, jnp.concatenate(cut(g_upper), axis=0))
-        pieces = pieces + mm(order_lower, jnp.concatenate(cut(g_lower), axis=0))
+        pieces = mm(order_out, jnp.concatenate([*cut_of(e_main, n), tail], axis=0))
         back_out[n * CHUNK : (n + 1) * CHUNK] = pieces.astype(BF16).reshape(CHUNK, PIECE, LANES)
     start_exchange(*back)
     back_in[me] = back_out[me]
 
-    gate_lines = iota((count, span), 1) - iota((count, span), 0) * PIECE
-    pick_lines = hot_of((gate_lines == gate_row) | (gate_lines == gate_row + 1))
+    gate_lines = iota((count, count * 8), 1) - iota((count, count * 8), 0) * 8
+    pick_lines = hot_of((gate_lines == 0) | (gate_lines == 1))
     lane, to = iota((LANES, depth * experts), 0), iota((LANES, depth * experts), 1)
     to_rank = over(to, experts)
     to_expert = to - to_rank * experts
@@ -533,9 +586,9 @@
     lax.fori_loop(1, dp_count, wait_row, 0)
     grouped = got_ref[...].astype(F32).reshape(dp_count * 8, 2 * LANES).astype(BF16)
 
-    wait_exchange(*back)
-    landed = back_in[...].reshape(span, LANES)
-    lines_upper, lines_lower = split_pair(mm(pick_lines, landed))
+    wait_exchange(*early_gate)
+    gate_lines = gate_in[...].astype(F32).reshape(count * 8, LANES).astype(BF16)
+    lines_upper, lines_lower = split_pair(mm(pick_lines, gate_lines))
     by_rank = mm(lines_upper, to_lane) + mm(lines_lower, to_lane)
     by_rank = jnp.sum(jnp.where(from_owner, by_rank, 0.0), axis=0, keepdims=True)
     picked = jnp.zeros((tokens, experts), F32)
@@ -558,7 +611,8 @@
     start_exchange(*term)
     term_in[me] = term_out[me]
 
-    mixed = mm(mix_ref[...], landed)
+    wait_exchange(*back)
+    mixed = mm(mix_ref[...], back_in[...].reshape(span, LANES))
     lane_of = over(iota((tokens, LANES), 1), TAIL)
     tails = jnp.zeros((tokens, LANES), F32)
     for e in range(local_experts):
@@ -589,6 +643,11 @@
     sums = jnp.sum(term_in[...], axis=0)
     grad_router_ref[:, :LANES] = sums[:local_experts]
     grad_router_ref[:, LANES:feature_share] = sums[local_experts : 2 * local_experts, :TAIL]
+
+
+def hand_over(grad_input_in, grad_router_in, grad_input_out, grad_router_out):
+    grad_input_out[0] = grad_input_in[...]
+    grad_router_out[...] = grad_router_in[...]
 
 
 def local(
@@ -621,16 +680,21 @@
     swaps = pltpu.SemaphoreType.DMA((parts,))
     peers = pltpu.SemaphoreType.DMA((count,))
     dp_peers = pltpu.SemaphoreType.DMA((dp_count,))
-    router_rows = jnp.pad(router_input[0], ((0, 8 - tokens // dp_count), (0, 0)))
     grad_input, grad_router = pl.pallas_call(
         functools.partial(layer_kernel, (count, ring, dp_1, local_experts, depth, parts)),
         out_shape=(
             jax.ShapeDtypeStruct((tokens, feature_share), BF16),
             jax.ShapeDtypeStruct((local_experts, feature_share), F32),
         ),
-        in_specs=[VMEM] * 5 + [HBM] * 5,
+        in_specs=[HBM] * 10,
         out_specs=(VMEM, VMEM),
         scratch_shapes=[
+            pltpu.VMEM((tokens, feature_share), BF16),
+            pltpu.VMEM(expert_ids.shape[:0:-1], jnp.int32),
+            pltpu.VMEM((tokens, experts), F32),
+            pltpu.VMEM(router_input.shape[1:], BF16),
+            pltpu.VMEM(router_weight.shape[::-1], BF16),
+            pltpu.VMEM((8, router_input.shape[2]), BF16),
             pltpu.VMEM((local_experts, 2 * LANES, width), BF16),
             pltpu.VMEM((local_experts, 2 * LANES, width), BF16),
             pltpu.VMEM((local_experts, 2 * LANES, width), BF16),
@@ -654,12 +718,15 @@
             pltpu.VMEM((expert_rows, LANES), F32),
             pltpu.VMEM((row_total, LANES), BF16),
             pltpu.VMEM((row_total, LANES), BF16),
+            pltpu.VMEM((count, 8, LANES), BF16),
+            pltpu.VMEM((count, 8, LANES), BF16),
             pltpu.VMEM((count, PIECE, LANES), BF16),
             pltpu.VMEM((count, PIECE, LANES), BF16),
             pltpu.VMEM(((local_experts + 1) * 2 * tokens, span), BF16),
             pltpu.VMEM((dp_count, 8, 2 * LANES), BF16),
             pltpu.VMEM((count, 8, LANES), F32),
             pltpu.VMEM((count, 8, LANES), F32),
+            pltpu.SemaphoreType.DMA((5,)),
             pltpu.SemaphoreType.DMA((3 * 2 * local_experts + 2,)),
             hops,
             hops,
@@ -667,6 +734,8 @@
             swaps,
             hops,
             hops,
+            peers,
+            peers,
             peers,
             peers,
             peers,
@@ -683,7 +752,7 @@
         grad_output[0],
         expert_ids[0].T,
         router_logits[0],
-        router_rows,
+        router_input[0],
         router_weight.T,
         gate_weight,
         up_weight,
@@ -691,7 +760,15 @@
         gate_saved.reshape(blocked),
         up_saved.reshape(blocked),
     )
-    return (grad_input[None], grad_router)
+    return pl.pallas_call(
+        hand_over,
+        out_shape=(
+            jax.ShapeDtypeStruct((1, tokens, feature_share), BF16),
+            jax.ShapeDtypeStruct((local_experts, feature_share), F32),
+        ),
+        in_specs=[VMEM, VMEM],
+        out_specs=(VMEM, VMEM),
+    )(grad_input, grad_router)
 
 
 def solution(mesh):

time: 103 us -> 98.5 us (0.956)
  local copies, waits for them, and re-layouts: 3.97 us -> 0 us
    unnamed x2 -> x0, local copies, waits for them, and re-layouts: 2.62 us -> none
    pallas_call x1, Pallas kernels: 98.4 us -> 96.3 us  [local(): pl.pallas_call(functools.partial(layer_kernel, (count, ring, dp_1, local_...]
    pallas_call x0 -> x1, Pallas kernels: none -> 1.35 us  [local(): pl.pallas_call(hand_over, out_shape=(jax.ShapeDtypeStruct((1, tokens, fea...]
    pad x1 -> x0, local copies, waits for them, and re-layouts: 1.35 us -> none  [local(): jnp.pad(router_input[0], ((0, 8 - tokens // dp_count), (0, 0)))]
where the time goes in v3:
time: 98.5 us; the launch traced here: 98.3 us
  Pallas kernels  97.6 us (99%)
    pallas_call x1, Pallas kernels, local(): pl.pallas_call(functools.partial(layer_kernel, (count, ring, dp_1, local_...  96.3 us

profile of v3, /device:TPU:1, one launch (start us, length us, event | category | flops | bytes accessed | tf_op | source)
XLA Modules:
  0.0 98.3 jit_solution(15601474504072945354)
XLA Ops:
  0.6 96.3 %shard_map.113 = (bf16[48,160]{1,0:T(8,128)(2,1)}, f32[4,160]{1,0:T(4,128)}) custom-call(bf16[48,160]{1,0:T(8,128)(2,1)} %bitcast.14, s32[8,48]{1,0:T(8,128)} %bitcast.17, f32[48,128]{1,0:T(8,128)} %bitcast.15, bf16[2,3840]{1,0:T(2,128)(2,1)} %bitcast.16, bf16[160,128]{1,0:T(8,128)(2,1)} %bitcast.13, bf16[4,160,1024]{2,1,0:T(8,128)(2,1)} %gate_hbm.1, ...), custom_call_target="tpu_custom_call" | custom-call | tf_op jit(solution)/shard_map/pallas_call | solution.py:683
  96.9 1.4 %shard_map.114 = (bf16[1,48,160]{2,1,0:T(8,128)(2,1)}, f32[4,160]{1,0:T(4,128)}) custom-call(bf16[48,160]{1,0:T(8,128)(2,1)} %get-tuple-element.4.grad_input_in, f32[4,160]{1,0:T(4,128)} %get-tuple-element.5.grad_router_in), custom_call_target="tpu_custom_call" | custom-call | tf_op jit(solution)/shard_map/pallas_call | solution.py:763

commit v4 on v3

--- a/solution.py
+++ b/solution.py
@@ -249,11 +249,12 @@
         )
 
     def start_exchange(*refs):
-        def start(k, carry):
-            exchange(k, *refs).start()
+        def start(n, carry):
+            away = (n + 1) // 2
+            exchange(count // 2 + away * (2 * lax.rem(n, 2) - 1), *refs).start()
             return carry
 
-        lax.fori_loop(1, count, start, 0)
+        lax.fori_loop(0, count - 1, start, 0)
 
     def wait_exchange(*refs):
         def wait(k, carry):

time: 98.5 us -> 96.3 us (0.978)
  Pallas kernels: 97.6 us -> 95.5 us
    pallas_call x1, Pallas kernels: 96.3 us -> 94.1 us  [local(): pl.pallas_call(functools.partial(layer_kernel, (count, ring, dp_1, local_...]
where the time goes in v4:
time: 96.3 us; the launch traced here: 96.1 us
  Pallas kernels  95.5 us (99%)
    pallas_call x1, Pallas kernels, local(): pl.pallas_call(functools.partial(layer_kernel, (count, ring, dp_1, local_...  94.1 us

profile of v4, /device:TPU:1, one launch (start us, length us, event | category | flops | bytes accessed | tf_op | source)
XLA Modules:
  0.0 96.1 jit_solution(10629828288045182388)
XLA Ops:
  0.6 94.1 %shard_map.113 = (bf16[48,160]{1,0:T(8,128)(2,1)}, f32[4,160]{1,0:T(4,128)}) custom-call(bf16[48,160]{1,0:T(8,128)(2,1)} %bitcast.14, s32[8,48]{1,0:T(8,128)} %bitcast.17, f32[48,128]{1,0:T(8,128)} %bitcast.15, bf16[2,3840]{1,0:T(2,128)(2,1)} %bitcast.16, bf16[160,128]{1,0:T(8,128)(2,1)} %bitcast.13, bf16[4,160,1024]{2,1,0:T(8,128)(2,1)} %gate_hbm.1, ...), custom_call_target="tpu_custom_call" | custom-call | tf_op jit(solution)/shard_map/pallas_call | solution.py:684
  94.8 1.4 %shard_map.114 = (bf16[1,48,160]{2,1,0:T(8,128)(2,1)}, f32[4,160]{1,0:T(4,128)}) custom-call(bf16[48,160]{1,0:T(8,128)(2,1)} %get-tuple-element.4.grad_input_in, f32[4,160]{1,0:T(4,128)} %get-tuple-element.5.grad_router_in), custom_call_target="tpu_custom_call" | custom-call | tf_op jit(solution)/shard_map/pallas_call | solution.py:764
